TPU v7x, 256 devices: a whole 4x4x8 slice. The times are simulated.
256 devices in a mesh: section: 4 (over x), vocab: 16 (over z, core), dp: 4 (over y).
Axes of the slice: x: 4, y: 4, z: 8, core: 2. Of those that a mesh axis runs over, the one named last changes fastest.
Arguments:
- hidden: bfloat16 [4, 1024, 3072], P('dp', ('section', 'vocab')), may hold values from -160 to 160
- head: bfloat16 [131072, 3072], P(('section', 'vocab')), may hold values from -3 to 3
- labels: int32 [4, 1024], P('dp'), may hold values from 0 to 131071
- response_mask: int32 [4, 1024], P('dp'), may hold values from 0 to 1, as said below
- seq_pair: int32 [4, 4], P('dp'), may hold values from 0 to 15, as said below
- ref_logp: float32 [16], replicated, may hold values from -12.6 to -12.4
Outputs:
- token_logprob: float32 [4, 1024], P('dp', ('section', 'vocab'))
- pair_margin: float32 [8], replicated
- loss: float32 [], replicated
Inputs may be any that keep to these rules, and one draw needn't show every extreme that they name: `response_mask`: each sequence of 256 rows has more than half of its rows set. `seq_pair`: over all replicas every slot of 0 to 15 appears once; slot q belongs to pair q // 2 and is its chosen response when q is even.
All inputs are finite; a program needn't handle non-finite values.
Results may differ from a plain program's by a relative error of at most 0.0003.
Values may be sent and summed in bfloat16 or wider, within the bound.
No kernel may reach another device: no remote copies, remote signals or barrier semaphores. Data moves between devices by JAX's collectives and lax.ppermute only.
A program may use at most 64 MiB of HBM per device.

v0:
```python
import functools

import jax
import jax.numpy as jnp
import numpy as np
from jax import lax
from jax.experimental import pallas as pl
from jax.experimental.pallas import tpu as pltpu
from jax.sharding import PartitionSpec as P


PLANE = ("section", "vocab")
beta_scale = 5.0

NS, NZ, NC = 4, 8, 2
TILE = 512


def place(s, z, c):
    return (s % NS) * NZ * NC + (z % NZ) * NC + c


def move(x, steps):
    pairs = [
        (place(s, z, c), place(s + steps[c][0], z + steps[c][1], c))
        for s in range(NS)
        for z in range(NZ)
        for c in range(NC)
        if steps[c] is not None
    ]
    return lax.ppermute(x, PLANE, pairs)


def swap_cores(x):
    pairs = [(p, p ^ 1) for p in range(NS * NZ * NC)]
    return lax.ppermute(x, PLANE, pairs)


XP, XM, ZP, ZM = (1, 0), (-1, 0), (0, 1), (0, -1)

QUADS_A = (0, -1, 1, -2, 2, -3, 3, 4)
QUADS_B = ((0, -1), (-1, -1), (1, -1), (2, -1), (1, 3), (-1, 3), (2, 3), (0, 3))


def join_kernel(*refs):
    for k in range(4):
        refs[4][pl.ds(16 * k, 16), :] = refs[k][...]


VMEM = pl.BlockSpec(memory_space=pltpu.VMEM)
SMALL = pltpu.CompilerParams(vmem_limit_bytes=4 * 1024 * 1024)


def held(*arrays):
    return [pltpu.with_memory_space_constraint(a, pltpu.VMEM) for a in arrays]


def join(*pieces):
    rows, width = pieces[0].shape
    return pl.pallas_call(
        join_kernel, in_specs=[VMEM] * 4, out_specs=VMEM, out_shape=pltpu.VMEM((4 * rows, width), pieces[0].dtype),
        compiler_params=SMALL,
    )(*held(*pieces))


def pick_kernel(first_ref, mine_ref, theirs_ref, out_ref):
    @pl.when(first_ref[0] == 1)
    def _():
        out_ref[...] = mine_ref[...]

    @pl.when(first_ref[0] != 1)
    def _():
        out_ref[...] = theirs_ref[...]


def pick(first, on_core_0, on_core_1):
    return pl.pallas_call(
        pick_kernel,
        in_specs=[pl.BlockSpec(memory_space=pltpu.SMEM), VMEM, VMEM],
        out_specs=VMEM,
        out_shape=pltpu.VMEM(on_core_0.shape, on_core_0.dtype),
        compiler_params=SMALL,
    )(first, *held(on_core_0, on_core_1))


def copy_kernel(in_ref, out_ref):
    out_ref[...] = in_ref[...]


def gather_quads(own, first, *small):
    kept = pl.pallas_call(
        copy_kernel, in_specs=[VMEM], out_specs=VMEM, out_shape=pltpu.VMEM(own.shape, own.dtype), compiler_params=SMALL
    )(own)
    r1p = move(own, (XP, ZP))
    r1m = move(own, (XM, ZM))
    r2m = move(r1m, (XM, ZM))
    r2p = move(r1p, (None, ZP))
    q0 = join(r1p, kept, r1m, r2m)
    q1p = move(q0, (ZP, XP))
    q1m = move(q0, (ZM, XM))
    q1p, *small = lax.optimization_barrier((q1p, *small))
    t3p = move(r2p, (None, ZP))
    t3m = move(r2m, (None, ZM))
    t4 = move(r2m, (None, (0, -2)))
    g2 = join(t3m, t4, t3p, r2p)
    q2p = move(q1p, (ZP, XP))
    q2m = move(pick(first, q1m, g2), (ZM, XM))
    q3p = move(pick(first, q2p, g2), (ZP, XP))
    q3m = move(q2m, (ZM, XM))
    q4 = move(q3p, (ZP, None))
    return (q0, q1p, q1m, q2p, q2m, q3p, q3m, q4, g2), small


def stats_kernel(*refs, pieces, heads, seeded):
    x_refs = refs[:pieces]
    target_ref = refs[pieces]
    head_refs = refs[pieces + 1 : pieces + 1 + heads]
    seed_ref = refs[pieces + 1 + heads] if seeded else None
    out_ref, rows_ref, tiles_ref, arrived = refs[-4:]
    step = pl.program_id(0)
    per_head = head_refs[0].shape[0] // TILE
    steps = heads * per_head
    slots = tiles_ref.shape[0]

    def fetch(k):
        slot = lax.rem(k, slots)
        for h in range(heads):

            @pl.when(k // per_head == h)
            def _():
                tile = head_refs[h].at[pl.ds((k - h * per_head) * TILE, TILE), :]
                pltpu.make_async_copy(tile, tiles_ref.at[slot], arrived.at[slot]).start()

    @pl.when(step == 0)
    def _():
        for k in range(slots - 1):
            fetch(k)
        for k in range(4):
            block = x_refs[k][...]
            if k == 3 and pieces == 5:
                block = block + x_refs[4][...]
            rows_ref[pl.ds(64 * k, 64), :] = block
        if seeded:
            out_ref[...] = seed_ref[...]
        else:
            out_ref[...] = jnp.zeros_like(out_ref)
            out_ref[0:1, :] = jnp.full((1, out_ref.shape[1]), -jnp.inf, jnp.float32)

    @pl.when(step + slots - 1 < steps)
    def _():
        fetch(step + slots - 1)

    slot = lax.rem(step, slots)
    pltpu.make_async_copy(tiles_ref.at[slot], tiles_ref.at[slot], arrived.at[slot]).wait()
    logits = lax.dot_general(
        tiles_ref[slot], rows_ref[...], (((1,), (1,)), ((), ())), preferred_element_type=jnp.float32
    )
    which = step // per_head
    target = target_ref[0:1, :] if heads == 1 else jnp.where(which == 0, target_ref[0:1, :], target_ref[1:2, :])
    old_max = out_ref[0:1, :]
    new_max = jnp.maximum(old_max, jnp.max(logits, axis=0, keepdims=True))
    index = lax.broadcasted_iota(jnp.int32, logits.shape, 0)
    hit = index == target - (step - which * per_head) * TILE
    picked = jnp.sum(jnp.where(hit, logits, 0.0), axis=0, keepdims=True)
    added = jnp.sum(jnp.exp(logits - new_max), axis=0, keepdims=True)
    out_ref[1:2, :] = out_ref[1:2, :] * jnp.exp(old_max - new_max) + added
    out_ref[2:3, :] = out_ref[2:3, :] + picked
    out_ref[0:1, :] = new_max


def chunk_stats(xs, targets, heads, seed=None):
    vocab_rows, width = heads[0].shape
    rows = targets.shape[1]
    ins = [*held(*xs), targets, *(pltpu.with_memory_space_constraint(h, pltpu.HBM) for h in heads)]
    whole = lambda a: pl.BlockSpec(a.shape, lambda i: (0,) * a.ndim)
    specs = [VMEM for x in xs] + [whole(targets)] + [pl.BlockSpec(memory_space=pltpu.HBM) for h in heads]
    if seed is not None:
        ins.append(seed)
        specs.append(whole(seed))
    work = len(heads) * vocab_rows
    return pl.pallas_call(
        functools.partial(stats_kernel, pieces=len(xs), heads=len(heads), seeded=seed is not None),
        grid=(work // TILE,),
        in_specs=specs,
        out_specs=pl.BlockSpec((8, rows), lambda i: (0, 0)),
        out_shape=jax.ShapeDtypeStruct((8, rows), jnp.float32),
        scratch_shapes=[
            pltpu.VMEM((rows, width), jnp.bfloat16),
            pltpu.VMEM((3, TILE, width), jnp.bfloat16),
            pltpu.SemaphoreType.DMA((3,)),
        ],
        cost_estimate=pl.CostEstimate(
            flops=2 * work * width * rows, bytes_accessed=2 * work * width, transcendentals=work * rows
        ),
        compiler_params=pltpu.CompilerParams(dimension_semantics=("arbitrary",), vmem_limit_bytes=32 * 1024 * 1024),
    )(*ins)


def copies(x, n):
    return jnp.broadcast_to(x, (n, *x.shape))


def combine(pieces):
    top = jnp.max(pieces[:, 0], axis=0)
    total = jnp.sum(pieces[:, 1] * jnp.exp(pieces[:, 0] - top), axis=0)
    return top, total, jnp.sum(pieces[:, 2], axis=0)


def step(hidden, head, labels, response_mask, seq_pair, ref_logp):
    rows = hidden.shape[1]
    vocab_rows = head.shape[0]
    s = lax.axis_index("section")
    zc = lax.axis_index("vocab")
    z, core = zc // NC, zc % NC
    first = core == 0
    position = lax.axis_index(PLANE)

    other_head = swap_cores(head)
    flag = jnp.reshape(1 - core, (1,))
    quads, (labels, response_mask, seq_pair) = gather_quads(hidden[0], flag, labels, response_mask, seq_pair)
    q0, q1p, q1m, q2p, q2m, q3p, q3m, q4, g2 = quads

    n = np.arange(8 * 4 * rows)
    quad, block, row = n // (4 * rows), n // rows % 4, n % rows
    ds_a, dz_a = block - 1, np.asarray(QUADS_A)[quad]
    ds_b, dz_b = np.asarray(QUADS_B)[quad, 0], block + np.asarray(QUADS_B)[quad, 1]
    to_s = (s + jnp.where(first, ds_a, ds_b)) % NS
    to_z = (z + jnp.where(first, dz_a, dz_b)) % NZ
    to = (to_s * NZ + to_z) * rows + row
    mine = lambda a: jnp.where(first, a[:, 0], a[:, 1]).reshape(-1)
    lab = mine(labels[0].reshape(NS * NZ, NC, rows))
    hit = n[:, None] == to[None, :]
    target = jnp.sum(jnp.where(hit, lab[:, None], 0), axis=0).reshape(2, 1, 4 * 4 * rows)
    target = target - jnp.stack([position, position ^ 1])[None, :, None] * vocab_rows

    early = (q0, q1p, q1m, q2p)
    late = (q2m, q3p, q3m, q4, g2)
    stats1 = chunk_stats(early, target[0, :1], [head])
    stats1 = chunk_stats(early, target[0, 1:], [other_head], stats1)
    stats2 = chunk_stats(late, target[1], [head, other_head])

    stats = jnp.concatenate([stats1, stats2], axis=1)
    stats = lax.dot_general(
        stats, hit.astype(jnp.float32), (((1,), (1,)), ((), ())), precision=lax.Precision.HIGHEST
    )[:3]

    same_core = [[NC * k + c for k in range(NS * NZ)] for c in range(NC)]
    pieces = lax.all_to_all(
        copies(stats, NS * NZ), PLANE, split_axis=0, concat_axis=0, tiled=True, axis_index_groups=same_core
    )
    top, total, label_logit = combine(pieces)
    logprob = label_logit - top - jnp.log(total)
    token_logprob = lax.dynamic_slice_in_dim(logprob, (s * NZ + z) * rows, rows)[None, :]

    slot_count = ref_logp.shape[0]
    weights = response_mask[0].astype(jnp.float32).reshape(NS, NZ * NC * rows)
    weights = weights / jnp.sum(weights, axis=1, keepdims=True)
    weights = mine(weights.reshape(NS * NZ, NC, rows))
    slots = jnp.broadcast_to(seq_pair[0][:, None], (NS, NZ * rows)).reshape(-1)
    slot_ids = lax.broadcasted_iota(jnp.int32, (slot_count, slots.shape[0]), 0)
    by_slot = jnp.where(slots[None, :] == slot_ids, weights[None, :], 0.0)
    part = jnp.sum(by_slot * logprob[None, :], axis=1)
    part = part + swap_cores(part)
    around = [lax.ppermute(part, "dp", [(i, (i + d) % 4) for i in range(4)]) for d in (1, 3, 2)]
    policy = part + around[0] + around[1] + around[2]
    pair_margin = beta_scale * (policy[0::2] - ref_logp[0::2] - (policy[1::2] - ref_logp[1::2]))
    loss = jnp.mean(jnp.logaddexp(0.0, -pair_margin))
    return (token_logprob, pair_margin, loss)


def solution(mesh):
    placed = (
        P("dp", PLANE, None),
        P(PLANE, None),
        P("dp", None),
        P("dp", None),
        P("dp", None),
        P(),
    )
    return jax.shard_map(
        step,
        mesh=mesh,
        in_specs=placed,
        out_specs=(P("dp", PLANE), P(), P()),
        check_vma=False,
    )
```

profile of v0, /device:TPU:1, one launch (start us, length us, event | category | flops | bytes accessed | tf_op | source)
XLA Modules:
  0.0 107.2 jit_solution(2093577954050485629)
XLA Ops:
  0.6 3.3 %collective-permute-start.6 = (bf16[2048,3072]{1,0:T(8,128)(2,1)}, bf16[2048,3072]{1,0:T(8,128)(2,1)}, u32[]{:S(2)}, u32[]{:S(2)}) collective-permute-start(bf16[2048,3072]{1,0:T(8,128)(2,1)} %refs_6_.1), channel_id=1, source_target_pairs={{0,4},{4,0},{8,12},{12,8},{16,20},{20,16},{24,28},{28,24},{32,36},... | collective-permute-start | bytes 37748744 | tf_op jit(solution)/shard_map/ppermute | solution.py:36
  3.9 3.9 %collective-permute-start.1 = (bf16[16,3072]{1,0:T(8,128)(2,1)}, bf16[16,3072]{1,0:T(8,128)(2,1)S(1)}, u32[]{:S(2)}, u32[]{:S(2)}) collective-permute-start(bf16[16,3072]{1,0:T(8,128)(2,1)} %bitcast.29), channel_id=1, source_target_pairs={{0,192},{4,60},{8,200},{12,4},{16,208},{20,12},{24,216},{28,20},{3... | collective-permute-start | bytes 294920 | tf_op jit(solution)/shard_map/ppermute | solution.py:31
  7.8 2.0 %collective-permute-done.1.refs_2_ = bf16[16,3072]{1,0:T(8,128)(2,1)S(1)} collective-permute-done((bf16[16,3072]{1,0:T(8,128)(2,1)}, bf16[16,3072]{1,0:T(8,128)(2,1)S(1)}, u32[]{:S(2)}, u32[]{:S(2)}) %collective-permute-start.1) | collective-permute-done | bytes 98336 | tf_op jit(solution)/shard_map/ppermute | solution.py:31
  9.8 2.9 %collective-permute-start.2 = (bf16[16,3072]{1,0:T(8,128)(2,1)S(1)}, bf16[16,3072]{1,0:T(8,128)(2,1)S(1)}, u32[]{:S(2)}, u32[]{:S(2)}) collective-permute-start(bf16[16,3072]{1,0:T(8,128)(2,1)S(1)} %collective-permute-done.1.refs_2_), channel_id=1, source_target_pairs={{0,192},{4,60},{8,200},{12,4},{16,208},{20,12},{24,216},{28,20},{3... | collective-permute-start | bytes 294920 | tf_op jit(solution)/shard_map/ppermute | solution.py:31
  14.4 1.3 %collective-permute-start.3 = (bf16[64,3072]{1,0:T(8,128)(2,1)S(1)}, bf16[64,3072]{1,0:T(8,128)(2,1)S(1)}, u32[]{:S(2)}, u32[]{:S(2)}) collective-permute-start(bf16[64,3072]{1,0:T(8,128)(2,1)S(1)} %shard_map.140.refs_0_), channel_id=1, source_target_pairs={{0,8},{4,68},{8,16},{12,76},{16,24},{20,84},{24,32},{28,92},{32,40... | collective-permute-start | bytes 1179656 | tf_op jit(solution)/shard_map/ppermute | solution.py:31
  15.7 1.9 %collective-permute-start.9 = (bf16[16,3072]{1,0:T(8,128)(2,1)S(1)}, bf16[16,3072]{1,0:T(8,128)(2,1)S(1)}, u32[]{:S(2)}, u32[]{:S(2)}) collective-permute-start(bf16[16,3072]{1,0:T(8,128)(2,1)S(1)} %collective-permute-done.refs_0_), channel_id=1, source_target_pairs={{4,12},{12,20},{20,28},{28,36},{36,44},{44,52},{52,60},{60,4},{68,... | collective-permute-start | bytes 294920 | tf_op jit(solution)/shard_map/ppermute | solution.py:31
  17.6 1.7 %collective-permute-start.4 = (bf16[64,3072]{1,0:T(8,128)(2,1)S(1)}, bf16[64,3072]{1,0:T(8,128)(2,1)S(1)}, u32[]{:S(2)}, u32[]{:S(2)}) collective-permute-start(bf16[64,3072]{1,0:T(8,128)(2,1)S(1)} %shard_map.140.refs_0_), channel_id=1, source_target_pairs={{0,56},{4,196},{8,0},{12,204},{16,8},{20,212},{24,16},{28,220},{32... | collective-permute-start | bytes 1179656 | tf_op jit(solution)/shard_map/ppermute | solution.py:31
  19.3 4.9 %collective-permute-start.7 = (bf16[16,3072]{1,0:T(8,128)(2,1)S(1)}, bf16[16,3072]{1,0:T(8,128)(2,1)S(1)}, u32[]{:S(2)}, u32[]{:S(2)}) collective-permute-start(bf16[16,3072]{1,0:T(8,128)(2,1)S(1)} %collective-permute-done.2.refs_3_), channel_id=1, source_target_pairs={{4,60},{12,4},{20,12},{28,20},{36,28},{44,36},{52,44},{60,52},{68,... | collective-permute-start | bytes 294920 | tf_op jit(solution)/shard_map/ppermute | solution.py:31
  26.4 3.1 %collective-permute-start.8 = (bf16[16,3072]{1,0:T(8,128)(2,1)S(1)}, bf16[16,3072]{1,0:T(8,128)(2,1)S(1)}, u32[]{:S(2)}, u32[]{:S(2)}) collective-permute-start(bf16[16,3072]{1,0:T(8,128)(2,1)S(1)} %collective-permute-done.2.refs_3_), channel_id=1, source_target_pairs={{4,52},{12,60},{20,4},{28,12},{36,20},{44,28},{52,36},{60,44},{68,... | collective-permute-start | bytes 294920 | tf_op jit(solution)/shard_map/ppermute | solution.py:31
  29.5 3.4 %collective-permute-start.10 = (bf16[16,3072]{1,0:T(8,128)(2,1)S(1)}, bf16[16,3072]{1,0:T(8,128)(2,1)S(1)}, u32[]{:S(2)}, u32[]{:S(2)}) collective-permute-start(bf16[16,3072]{1,0:T(8,128)(2,1)S(1)} %collective-permute-done.9.refs_3_), channel_id=1, source_target_pairs={{4,12},{12,20},{20,28},{28,36},{36,44},{44,52},{52,60},{60,4},{68,... | collective-permute-start | bytes 294920 | tf_op jit(solution)/shard_map/ppermute | solution.py:31
  34.0 3.4 %collective-permute-done.10.refs_2_ = bf16[16,3072]{1,0:T(8,128)(2,1)S(1)} collective-permute-done((bf16[16,3072]{1,0:T(8,128)(2,1)S(1)}, bf16[16,3072]{1,0:T(8,128)(2,1)S(1)}, u32[]{:S(2)}, u32[]{:S(2)}) %collective-permute-start.10) | collective-permute-done | bytes 98336 | tf_op jit(solution)/shard_map/ppermute | solution.py:31
  38.0 1.3 %reduce.19 = s32[1024]{0:T(1024)S(1)} reduce(s32[1,1024]{1,0:T(1,128)} %param.14, s32[]{:T(128)} %broadcast.63), dimensions={0}, to_apply=%get-tuple-element.8.reduce_sub_computation.3 | reduce | bytes 8196 | tf_op jit(solution)/shard_map/optimization_barrier | solution.py:101
  39.9 2.7 %collective-permute-start.11 = (bf16[64,3072]{1,0:T(8,128)(2,1)S(1)}, bf16[64,3072]{1,0:T(8,128)(2,1)S(1)}, u32[]{:S(2)}, u32[]{:S(2)}) collective-permute-start(bf16[64,3072]{1,0:T(8,128)(2,1)S(1)} %shard_map.144), channel_id=1, source_target_pairs={{0,56},{4,196},{8,0},{12,204},{16,8},{20,212},{24,16},{28,220},{32... | collective-permute-start | bytes 1179656 | tf_op jit(solution)/shard_map/ppermute | solution.py:31
  44.5 2.9 %collective-permute-done.5.refs_3_.mine_ref = bf16[64,3072]{1,0:T(8,128)(2,1)S(1)} collective-permute-done((bf16[64,3072]{1,0:T(8,128)(2,1)S(1)}, bf16[64,3072]{1,0:T(8,128)(2,1)S(1)}, u32[]{:S(2)}, u32[]{:S(2)}) %collective-permute-start.5) | collective-permute-done | bytes 393248 | tf_op jit(solution)/shard_map/ppermute | solution.py:31
  47.6 2.9 %collective-permute-start.13 = (bf16[64,3072]{1,0:T(8,128)(2,1)S(1)}, bf16[64,3072]{1,0:T(8,128)(2,1)S(1)}, u32[]{:S(2)}, u32[]{:S(2)}) collective-permute-start(bf16[64,3072]{1,0:T(8,128)(2,1)S(1)} %collective-permute-done.11.refs_0_), channel_id=1, source_target_pairs={{0,56},{4,196},{8,0},{12,204},{16,8},{20,212},{24,16},{28,220},{32... | collective-permute-start | bytes 1179656 | tf_op jit(solution)/shard_map/ppermute | solution.py:31
  50.5 5.2 %collective-permute-done.12.refs_1_ = bf16[64,3072]{1,0:T(8,128)(2,1)S(1)} collective-permute-done((bf16[64,3072]{1,0:T(8,128)(2,1)S(1)}, bf16[64,3072]{1,0:T(8,128)(2,1)S(1)}, u32[]{:S(2)}, u32[]{:S(2)}) %collective-permute-start.12) | collective-permute-done | bytes 393248 | tf_op jit(solution)/shard_map/ppermute | solution.py:31
  56.4 6.5 %shard_map.141.refs_6_ = f32[8,256]{1,0:T(8,128)S(1)} custom-call(bf16[64,3072]{1,0:T(8,128)(2,1)S(1)} %shard_map.140.refs_0_, bf16[64,3072]{1,0:T(8,128)(2,1)S(1)} %collective-permute-done.3.refs_1_, bf16[64,3072]{1,0:T(8,128)(2,1)S(1)} %collective-permute-done.4.refs_2_.mine_ref, bf16[64,3072]{1,0:T(8,128)(2,1)S(1)} %collective-permute-done.5.refs_3_.mine_ref, ...), custom_call_target="tpu_custom_call" | custom-call | flops 3221225472 | bytes 12582912 | tf_op jit(solution)/shard_map/pallas_call | solution.py:181
  62.9 6.5 %shard_map.142 = f32[8,256]{1,0:T(8,128)S(1)} custom-call(bf16[64,3072]{1,0:T(8,128)(2,1)S(1)} %shard_map.140.refs_0_, bf16[64,3072]{1,0:T(8,128)(2,1)S(1)} %collective-permute-done.3.refs_1_, bf16[64,3072]{1,0:T(8,128)(2,1)S(1)} %collective-permute-done.4.refs_2_.mine_ref, bf16[64,3072]{1,0:T(8,128)(2,1)S(1)} %collective-permute-done.5.refs_3_.mine_ref, ...), custom_call_target="tpu_custom_call" | custom-call | flops 3221225472 | bytes 12582912 | tf_op jit(solution)/shard_map/pallas_call | solution.py:181
  69.4 11.0 %shard_map.146 = f32[8,256]{1,0:T(8,128)S(1)} custom-call(bf16[64,3072]{1,0:T(8,128)(2,1)S(1)} %collective-permute-done.11.refs_0_, bf16[64,3072]{1,0:T(8,128)(2,1)S(1)} %collective-permute-done.12.refs_1_, bf16[64,3072]{1,0:T(8,128)(2,1)S(1)} %collective-permute-done.13.refs_2_, bf16[64,3072]{1,0:T(8,128)(2,1)S(1)} %collective-permute-done.14.refs_3_, ...), custom_call_target="tpu_custom_call" | custom-call | flops 6442450944 | bytes 25165824 | tf_op jit(solution)/shard_map/pallas_call | solution.py:181
  81.7 4.0 %all-to-all-start = ((f32[32,3,512]{2,1,0:T(4,128)}), f32[32,3,512]{2,1,0:T(4,128)S(1)}, u32[]{:S(2)}, u32[]{:S(2)}) async-start(f32[32,3,512]{2,1,0:T(4,128)} %broadcast_in_dim.44), calls=%async_computation | async-start | bytes 524288 | tf_op jit(solution)/shard_map/all_to_all | solution.py:248
  86.1 9.7 %all-to-all-done = f32[32,3,512]{2,1,0:T(4,128)S(1)} async-done(((f32[32,3,512]{2,1,0:T(4,128)}), f32[32,3,512]{2,1,0:T(4,128)S(1)}, u32[]{:S(2)}, u32[]{:S(2)}) %all-to-all-start) | async-done | bytes 196640 | tf_op jit(solution)/shard_map/all_to_all | solution.py:248
  98.7 1.4 %collective-permute-start.17 = (f32[16]{0:T(128)S(1)}, f32[16]{0:T(128)S(1)}, u32[]{:S(2)}, u32[]{:S(2)}) collective-permute-start(f32[16]{0:T(128)S(1)} %add.69), channel_id=1, source_target_pairs={{0,3},{1,0},{2,1},{3,2},{4,7},{5,4},{6,5},{7,6},{8,11},{9,8},{10,9... | collective-permute-start | bytes 200 | tf_op jit(solution)/shard_map/ppermute | solution.py:264
  100.2 1.6 %collective-permute-start.18 = (f32[16]{0:T(128)S(1)}, f32[16]{0:T(128)S(1)}, u32[]{:S(2)}, u32[]{:S(2)}) collective-permute-start(f32[16]{0:T(128)S(1)} %add.69), channel_id=1, source_target_pairs={{0,2},{1,3},{2,0},{3,1},{4,6},{5,7},{6,4},{7,5},{8,10},{9,11},{10,... | collective-permute-start | bytes 200 | tf_op jit(solution)/shard_map/ppermute | solution.py:264
  101.8 2.3 %collective-permute-done.18 = f32[16]{0:T(128)S(1)} collective-permute-done((f32[16]{0:T(128)S(1)}, f32[16]{0:T(128)S(1)}, u32[]{:S(2)}, u32[]{:S(2)}) %collective-permute-start.18) | collective-permute-done | bytes 96 | tf_op jit(solution)/shard_map/ppermute | solution.py:264
  (65 shorter events, 14.6 us)
Async XLA Ops:
  0.6 85.4 %copy-start = (s32[1,4]{1,0:T(1,128)S(1)}, s32[1,4]{1,0:T(1,128)}, u32[]{:S(2)}) copy-start(s32[1,4]{1,0:T(1,128)} %param.16) | copy-start | bytes 52
  0.6 62.2 %collective-permute-start.6 = (bf16[2048,3072]{1,0:T(8,128)(2,1)}, bf16[2048,3072]{1,0:T(8,128)(2,1)}, u32[]{:S(2)}, u32[]{:S(2)}) collective-permute-start(bf16[2048,3072]{1,0:T(8,128)(2,1)} %refs_6_.1), channel_id=1, source_target_pairs={{0,4},{4,0},{8,12},{12,8},{16,20},{20,16},{24,28},{28,24},{32,36},... | collective-permute-start | bytes 37748744 | tf_op jit(solution)/shard_map/ppermute | solution.py:36
  3.9 5.8 %collective-permute-start.1 = (bf16[16,3072]{1,0:T(8,128)(2,1)}, bf16[16,3072]{1,0:T(8,128)(2,1)S(1)}, u32[]{:S(2)}, u32[]{:S(2)}) collective-permute-start(bf16[16,3072]{1,0:T(8,128)(2,1)} %bitcast.29), channel_id=1, source_target_pairs={{0,192},{4,60},{8,200},{12,4},{16,208},{20,12},{24,216},{28,20},{3... | collective-permute-start | bytes 294920 | tf_op jit(solution)/shard_map/ppermute | solution.py:31
  7.8 5.8 %collective-permute-start = (bf16[16,3072]{1,0:T(8,128)(2,1)}, bf16[16,3072]{1,0:T(8,128)(2,1)S(1)}, u32[]{:S(2)}, u32[]{:S(2)}) collective-permute-start(bf16[16,3072]{1,0:T(8,128)(2,1)} %bitcast.30), channel_id=1, source_target_pairs={{0,64},{4,12},{8,72},{12,20},{16,80},{20,28},{24,88},{28,36},{32,9... | collective-permute-start | bytes 294920 | tf_op jit(solution)/shard_map/ppermute | solution.py:31
  9.8 4.6 %collective-permute-start.2 = (bf16[16,3072]{1,0:T(8,128)(2,1)S(1)}, bf16[16,3072]{1,0:T(8,128)(2,1)S(1)}, u32[]{:S(2)}, u32[]{:S(2)}) collective-permute-start(bf16[16,3072]{1,0:T(8,128)(2,1)S(1)} %collective-permute-done.1.refs_2_), channel_id=1, source_target_pairs={{0,192},{4,60},{8,200},{12,4},{16,208},{20,12},{24,216},{28,20},{3... | collective-permute-start | bytes 294920 | tf_op jit(solution)/shard_map/ppermute | solution.py:31
  12.7 0.9 copy-start.1
  14.4 23.1 %collective-permute-start.3 = (bf16[64,3072]{1,0:T(8,128)(2,1)S(1)}, bf16[64,3072]{1,0:T(8,128)(2,1)S(1)}, u32[]{:S(2)}, u32[]{:S(2)}) collective-permute-start(bf16[64,3072]{1,0:T(8,128)(2,1)S(1)} %shard_map.140.refs_0_), channel_id=1, source_target_pairs={{0,8},{4,68},{8,16},{12,76},{16,24},{20,84},{24,32},{28,92},{32,40... | collective-permute-start | bytes 1179656 | tf_op jit(solution)/shard_map/ppermute | solution.py:31
  15.7 10.8 %collective-permute-start.9 = (bf16[16,3072]{1,0:T(8,128)(2,1)S(1)}, bf16[16,3072]{1,0:T(8,128)(2,1)S(1)}, u32[]{:S(2)}, u32[]{:S(2)}) collective-permute-start(bf16[16,3072]{1,0:T(8,128)(2,1)S(1)} %collective-permute-done.refs_0_), channel_id=1, source_target_pairs={{4,12},{12,20},{20,28},{28,36},{36,44},{44,52},{52,60},{60,4},{68,... | collective-permute-start | bytes 294920 | tf_op jit(solution)/shard_map/ppermute | solution.py:31
  17.6 22.3 %collective-permute-start.4 = (bf16[64,3072]{1,0:T(8,128)(2,1)S(1)}, bf16[64,3072]{1,0:T(8,128)(2,1)S(1)}, u32[]{:S(2)}, u32[]{:S(2)}) collective-permute-start(bf16[64,3072]{1,0:T(8,128)(2,1)S(1)} %shard_map.140.refs_0_), channel_id=1, source_target_pairs={{0,56},{4,196},{8,0},{12,204},{16,8},{20,212},{24,16},{28,220},{32... | collective-permute-start | bytes 1179656 | tf_op jit(solution)/shard_map/ppermute | solution.py:31
  19.3 10.3 %collective-permute-start.7 = (bf16[16,3072]{1,0:T(8,128)(2,1)S(1)}, bf16[16,3072]{1,0:T(8,128)(2,1)S(1)}, u32[]{:S(2)}, u32[]{:S(2)}) collective-permute-start(bf16[16,3072]{1,0:T(8,128)(2,1)S(1)} %collective-permute-done.2.refs_3_), channel_id=1, source_target_pairs={{4,60},{12,4},{20,12},{28,20},{36,28},{44,36},{52,44},{60,52},{68,... | collective-permute-start | bytes 294920 | tf_op jit(solution)/shard_map/ppermute | solution.py:31
  26.4 7.6 %collective-permute-start.8 = (bf16[16,3072]{1,0:T(8,128)(2,1)S(1)}, bf16[16,3072]{1,0:T(8,128)(2,1)S(1)}, u32[]{:S(2)}, u32[]{:S(2)}) collective-permute-start(bf16[16,3072]{1,0:T(8,128)(2,1)S(1)} %collective-permute-done.2.refs_3_), channel_id=1, source_target_pairs={{4,52},{12,60},{20,4},{28,12},{36,20},{44,28},{52,36},{60,44},{68,... | collective-permute-start | bytes 294920 | tf_op jit(solution)/shard_map/ppermute | solution.py:31
  29.5 7.9 %collective-permute-start.10 = (bf16[16,3072]{1,0:T(8,128)(2,1)S(1)}, bf16[16,3072]{1,0:T(8,128)(2,1)S(1)}, u32[]{:S(2)}, u32[]{:S(2)}) collective-permute-start(bf16[16,3072]{1,0:T(8,128)(2,1)S(1)} %collective-permute-done.9.refs_3_), channel_id=1, source_target_pairs={{4,12},{12,20},{20,28},{28,36},{36,44},{44,52},{52,60},{60,4},{68,... | collective-permute-start | bytes 294920 | tf_op jit(solution)/shard_map/ppermute | solution.py:31
  39.6 7.9 %collective-permute-start.5 = (bf16[64,3072]{1,0:T(8,128)(2,1)S(1)}, bf16[64,3072]{1,0:T(8,128)(2,1)S(1)}, u32[]{:S(2)}, u32[]{:S(2)}) collective-permute-start(bf16[64,3072]{1,0:T(8,128)(2,1)S(1)} %collective-permute-done.3.refs_1_), channel_id=1, source_target_pairs={{0,8},{4,68},{8,16},{12,76},{16,24},{20,84},{24,32},{28,92},{32,40... | collective-permute-start | bytes 1179656 | tf_op jit(solution)/shard_map/ppermute | solution.py:31
  39.9 7.7 %collective-permute-start.11 = (bf16[64,3072]{1,0:T(8,128)(2,1)S(1)}, bf16[64,3072]{1,0:T(8,128)(2,1)S(1)}, u32[]{:S(2)}, u32[]{:S(2)}) collective-permute-start(bf16[64,3072]{1,0:T(8,128)(2,1)S(1)} %shard_map.144), channel_id=1, source_target_pairs={{0,56},{4,196},{8,0},{12,204},{16,8},{20,212},{24,16},{28,220},{32... | collective-permute-start | bytes 1179656 | tf_op jit(solution)/shard_map/ppermute | solution.py:31
  47.5 8.2 %collective-permute-start.12 = (bf16[64,3072]{1,0:T(8,128)(2,1)S(1)}, bf16[64,3072]{1,0:T(8,128)(2,1)S(1)}, u32[]{:S(2)}, u32[]{:S(2)}) collective-permute-start(bf16[64,3072]{1,0:T(8,128)(2,1)S(1)} %shard_map.145), channel_id=1, source_target_pairs={{0,8},{4,68},{8,16},{12,76},{16,24},{20,84},{24,32},{28,92},{32,40... | collective-permute-start | bytes 1179656 | tf_op jit(solution)/shard_map/ppermute | solution.py:31
  47.6 21.7 %collective-permute-start.13 = (bf16[64,3072]{1,0:T(8,128)(2,1)S(1)}, bf16[64,3072]{1,0:T(8,128)(2,1)S(1)}, u32[]{:S(2)}, u32[]{:S(2)}) collective-permute-start(bf16[64,3072]{1,0:T(8,128)(2,1)S(1)} %collective-permute-done.11.refs_0_), channel_id=1, source_target_pairs={{0,56},{4,196},{8,0},{12,204},{16,8},{20,212},{24,16},{28,220},{32... | collective-permute-start | bytes 1179656 | tf_op jit(solution)/shard_map/ppermute | solution.py:31
  55.7 13.7 %collective-permute-start.14 = (bf16[64,3072]{1,0:T(8,128)(2,1)S(1)}, bf16[64,3072]{1,0:T(8,128)(2,1)S(1)}, u32[]{:S(2)}, u32[]{:S(2)}) collective-permute-start(bf16[64,3072]{1,0:T(8,128)(2,1)S(1)} %collective-permute-done.12.refs_1_), channel_id=1, source_target_pairs={{0,8},{8,16},{16,24},{24,32},{32,40},{40,48},{48,56},{56,0},{64,72... | collective-permute-start | bytes 1179656 | tf_op jit(solution)/shard_map/ppermute | solution.py:31
  81.7 14.1 %all-to-all-start = ((f32[32,3,512]{2,1,0:T(4,128)}), f32[32,3,512]{2,1,0:T(4,128)S(1)}, u32[]{:S(2)}, u32[]{:S(2)}) async-start(f32[32,3,512]{2,1,0:T(4,128)} %broadcast_in_dim.44), calls=%async_computation | async-start | bytes 524288 | tf_op jit(solution)/shard_map/all_to_all | solution.py:248
  96.2 1.2 %collective-permute-start.15 = (f32[16]{0:T(128)S(1)}, f32[16]{0:T(128)S(1)}, u32[]{:S(2)}, u32[]{:S(2)}) collective-permute-start(f32[16]{0:T(128)S(1)} %multiply_reduce_fusion), channel_id=1, source_target_pairs={{0,4},{4,0},{8,12},{12,8},{16,20},{20,16},{24,28},{28,24},{32,36},... | collective-permute-start | bytes 200 | tf_op jit(solution)/shard_map/ppermute | solution.py:36
  97.4 4.4 %collective-permute-start.16 = (f32[16]{0:T(128)S(1)}, f32[16]{0:T(128)S(1)}, u32[]{:S(2)}, u32[]{:S(2)}) collective-permute-start(f32[16]{0:T(128)S(1)} %add.69), channel_id=1, source_target_pairs={{0,1},{1,2},{2,3},{3,0},{4,5},{5,6},{6,7},{7,4},{8,9},{9,10},{10,1... | collective-permute-start | bytes 200 | tf_op jit(solution)/shard_map/ppermute | solution.py:264
  98.7 3.1 %collective-permute-start.17 = (f32[16]{0:T(128)S(1)}, f32[16]{0:T(128)S(1)}, u32[]{:S(2)}, u32[]{:S(2)}) collective-permute-start(f32[16]{0:T(128)S(1)} %add.69), channel_id=1, source_target_pairs={{0,3},{1,0},{2,1},{3,2},{4,7},{5,4},{6,5},{7,6},{8,11},{9,8},{10,9... | collective-permute-start | bytes 200 | tf_op jit(solution)/shard_map/ppermute | solution.py:264
  100.2 3.9 %collective-permute-start.18 = (f32[16]{0:T(128)S(1)}, f32[16]{0:T(128)S(1)}, u32[]{:S(2)}, u32[]{:S(2)}) collective-permute-start(f32[16]{0:T(128)S(1)} %add.69), channel_id=1, source_target_pairs={{0,2},{1,3},{2,0},{3,1},{4,6},{5,7},{6,4},{7,5},{8,10},{9,11},{10,... | collective-permute-start | bytes 200 | tf_op jit(solution)/shard_map/ppermute | solution.py:264
where the time goes:
time: 108 us; the launch traced here: 107 us
  starting transfers between devices  41.3 us (38%)
  waiting for transfers between devices  27.9 us (26%)
  Pallas kernels  24.1 us (22%)
  other arithmetic  5.66 us (5%)
  local copies, waits for them, and re-layouts  5.04 us (5%)
  between operations  2.68 us (2%)
    ppermute x14, starting transfers between devices, move(): return lax.ppermute(x, PLANE, pairs)  29.5 us
    pallas_call x3, Pallas kernels, chunk_stats(): pl.pallas_call(functools.partial(stats_kernel, pieces=len(xs), heads=len(...  23.9 us
    ppermute x14, waiting for transfers between devices, move(): return lax.ppermute(x, PLANE, pairs)  15.3 us
    all_to_all x1, waiting for transfers between devices, step(): lax.all_to_all(copies(stats, NS * NZ), PLANE, split_axis=0, concat_axis=0...  9.75 us
    ppermute x3, starting transfers between devices, step(): lax.ppermute(part, 'dp', [(i, (i + d) % 4) for i in range(4)])  4.37 us
    all_to_all x1, starting transfers between devices, step(): lax.all_to_all(copies(stats, NS * NZ), PLANE, split_axis=0, concat_axis=0...  4.05 us
    ppermute x2, starting transfers between devices, swap_cores(): return lax.ppermute(x, PLANE, pairs)  3.38 us
    ppermute x3, waiting for transfers between devices, step(): lax.ppermute(part, 'dp', [(i, (i + d) % 4) for i in range(4)])  2.28 us
  transfers between devices with their start and end apart: 20, of which 9 were waited for; matrix products, arithmetic and copies ran while one was open for 7% of the time, Pallas kernels for 12%

commit v1 on v0

--- a/solution.py
+++ b/solution.py
@@ -38,13 +38,14 @@
 
 XP, XM, ZP, ZM = (1, 0), (-1, 0), (0, 1), (0, -1)
 
-QUADS_A = (0, -1, 1, -2, 2, -3, 3, 4)
-QUADS_B = ((0, -1), (-1, -1), (1, -1), (2, -1), (1, 3), (-1, 3), (2, 3), (0, 3))
+QUADS_A = (0, -1, 1, -2, -3, 3, 4, 2)
+QUADS_B = ((0, -1), (-1, -1), (1, -1), (2, -1), (-1, 3), (1, 3), (2, 3), (0, 3))
 
 
 def join_kernel(*refs):
-    for k in range(4):
-        refs[4][pl.ds(16 * k, 16), :] = refs[k][...]
+    k, rows = len(refs) - 1, refs[0].shape[0]
+    for i in range(k):
+        refs[k][pl.ds(rows * i, rows), :] = refs[i][...]
 
 
 VMEM = pl.BlockSpec(memory_space=pltpu.VMEM)
@@ -58,7 +59,10 @@
 def join(*pieces):
     rows, width = pieces[0].shape
     return pl.pallas_call(
-        join_kernel, in_specs=[VMEM] * 4, out_specs=VMEM, out_shape=pltpu.VMEM((4 * rows, width), pieces[0].dtype),
+        join_kernel,
+        in_specs=[VMEM] * len(pieces),
+        out_specs=VMEM,
+        out_shape=pltpu.VMEM((len(pieces) * rows, width), pieces[0].dtype),
         compiler_params=SMALL,
     )(*held(*pieces))
 
@@ -94,21 +98,20 @@
     r1p = move(own, (XP, ZP))
     r1m = move(own, (XM, ZM))
     r2m = move(r1m, (XM, ZM))
-    r2p = move(r1p, (None, ZP))
-    q0 = join(r1p, kept, r1m, r2m)
+    behind, ahead = join(r1p, kept), join(r1m, r2m)
+    q0 = join(behind, ahead)
     q1p = move(q0, (ZP, XP))
     q1m = move(q0, (ZM, XM))
+    f3 = move(ahead, (None, (0, -2)))
+    f5 = move(behind, (None, (0, 2)))
     q1p, *small = lax.optimization_barrier((q1p, *small))
-    t3p = move(r2p, (None, ZP))
-    t3m = move(r2m, (None, ZM))
-    t4 = move(r2m, (None, (0, -2)))
-    g2 = join(t3m, t4, t3p, r2p)
     q2p = move(q1p, (ZP, XP))
-    q2m = move(pick(first, q1m, g2), (ZM, XM))
-    q3p = move(pick(first, q2p, g2), (ZP, XP))
-    q3m = move(q2m, (ZM, XM))
-    q4 = move(q3p, (ZP, None))
-    return (q0, q1p, q1m, q2p, q2m, q3p, q3m, q4, g2), small
+    q2m = move(q1m, (ZM, None))
+    far = join(f3, f5)
+    q3p = move(pick(first, q2p, far), (ZP, XP))
+    q3m = move(pick(first, q2m, far), (ZM, XM))
+    q4 = move(q3p, (ZP, XP))
+    return (q0, q1p, q1m, q2p, q3p, q3m, q4, q2m, far), small
 
 
 def stats_kernel(*refs, pieces, heads, seeded):
@@ -217,8 +220,9 @@
 
     other_head = swap_cores(head)
     flag = jnp.reshape(1 - core, (1,))
-    quads, (labels, response_mask, seq_pair) = gather_quads(hidden[0], flag, labels, response_mask, seq_pair)
-    q0, q1p, q1m, q2p, q2m, q3p, q3m, q4, g2 = quads
+    quads, (labels, s, z, core) = gather_quads(hidden[0], flag, labels, s, z, core)
+    first = core == 0
+    early, late = quads[:4], quads[4:]
 
     n = np.arange(8 * 4 * rows)
     quad, block, row = n // (4 * rows), n // rows % 4, n % rows
@@ -233,8 +237,6 @@
     target = jnp.sum(jnp.where(hit, lab[:, None], 0), axis=0).reshape(2, 1, 4 * 4 * rows)
     target = target - jnp.stack([position, position ^ 1])[None, :, None] * vocab_rows
 
-    early = (q0, q1p, q1m, q2p)
-    late = (q2m, q3p, q3m, q4, g2)
     stats1 = chunk_stats(early, target[0, :1], [head])
     stats1 = chunk_stats(early, target[0, 1:], [other_head], stats1)
     stats2 = chunk_stats(late, target[1], [head, other_head])
@@ -245,9 +247,9 @@
     )[:3]
 
     same_core = [[NC * k + c for k in range(NS * NZ)] for c in range(NC)]
-    pieces = lax.all_to_all(
-        copies(stats, NS * NZ), PLANE, split_axis=0, concat_axis=0, tiled=True, axis_index_groups=same_core
-    )
+    stats, response_mask, seq_pair, ref_logp = lax.optimization_barrier((stats, response_mask, seq_pair, ref_logp))
+    sent = copies(stats, NS * NZ)
+    pieces = lax.all_to_all(sent, PLANE, split_axis=0, concat_axis=0, tiled=True, axis_index_groups=same_core)
     top, total, label_logit = combine(pieces)
     logprob = label_logit - top - jnp.log(total)
     token_logprob = lax.dynamic_slice_in_dim(logprob, (s * NZ + z) * rows, rows)[None, :]

time: 108 us -> 107 us (level)
  waiting for transfers between devices: 27.9 us -> 30.6 us
  other arithmetic: 5.66 us -> 4.31 us
  local copies, waits for them, and re-layouts: 5.04 us -> 3.73 us
  starting transfers between devices: 41.3 us -> 40 us
    ppermute x14 -> x12, starting transfers between devices: 29.5 us -> 20.7 us  [move(): return lax.ppermute(x, PLANE, pairs)]
    ppermute x14 -> x12, waiting for transfers between devices: 15.3 us -> 19.1 us  [move(): return lax.ppermute(x, PLANE, pairs)]
    all_to_all x1, starting transfers between devices: 4.05 us -> 7.83 us  [step(): lax.all_to_all(sent, PLANE, split_axis=0, concat_axis=0, tiled=True, axis...]
    ppermute x2, starting transfers between devices: 3.38 us -> 7.11 us  [swap_cores(): return lax.ppermute(x, PLANE, pairs)]
    convert_element_type x2, other arithmetic: 1.39 us -> 0.03 us  [step(): weights = response_mask[0].astype(jnp.float32).reshape(NS, NZ * NC * rows)]
  transfers between devices with their start and end apart: 20 -> 18, of which waited for: 9 -> 9; matrix products, arithmetic and copies ran while one was open for 7% -> 4% of each run, Pallas kernels for 12% -> 12%
where the time goes in v1:
time: 107 us; the launch traced here: 106 us
  starting transfers between devices  40 us (37%)
  waiting for transfers between devices  30.6 us (29%)
  Pallas kernels  24.1 us (23%)
  other arithmetic  4.31 us (4%)
  local copies, waits for them, and re-layouts  3.73 us (3%)
  between operations  2.74 us (3%)
    pallas_call x3, Pallas kernels, chunk_stats(): pl.pallas_call(functools.partial(stats_kernel, pieces=len(xs), heads=len(...  23.9 us
    ppermute x12, starting transfers between devices, move(): return lax.ppermute(x, PLANE, pairs)  20.7 us
    ppermute x12, waiting for transfers between devices, move(): return lax.ppermute(x, PLANE, pairs)  19.1 us
    all_to_all x1, waiting for transfers between devices, step(): lax.all_to_all(sent, PLANE, split_axis=0, concat_axis=0, tiled=True, axis...  8.94 us
    all_to_all x1, starting transfers between devices, step(): lax.all_to_all(sent, PLANE, split_axis=0, concat_axis=0, tiled=True, axis...  7.83 us
    ppermute x2, starting transfers between devices, swap_cores(): return lax.ppermute(x, PLANE, pairs)  7.11 us
    ppermute x3, starting transfers between devices, step(): lax.ppermute(part, 'dp', [(i, (i + d) % 4) for i in range(4)])  4.38 us
    ppermute x3, waiting for transfers between devices, step(): lax.ppermute(part, 'dp', [(i, (i + d) % 4) for i in range(4)])  2.28 us
  transfers between devices with their start and end apart: 18, of which 9 were waited for; matrix products, arithmetic and copies ran while one was open for 4% of the time, Pallas kernels for 12%

profile of v1, /device:TPU:1, one launch (start us, length us, event | category | flops | bytes accessed | tf_op | source)
XLA Modules:
  0.0 106.0 jit_solution(1992539541291585556)
XLA Ops:
  0.6 3.3 %collective-permute-start.6 = (bf16[2048,3072]{1,0:T(8,128)(2,1)}, bf16[2048,3072]{1,0:T(8,128)(2,1)}, u32[]{:S(2)}, u32[]{:S(2)}) collective-permute-start(bf16[2048,3072]{1,0:T(8,128)(2,1)} %refs_6_.1), channel_id=1, source_target_pairs={{0,4},{4,0},{8,12},{12,8},{16,20},{20,16},{24,28},{28,24},{32,36},... | collective-permute-start | bytes 37748744 | tf_op jit(solution)/shard_map/ppermute | solution.py:36
  3.9 3.9 %collective-permute-start.1 = (bf16[16,3072]{1,0:T(8,128)(2,1)}, bf16[16,3072]{1,0:T(8,128)(2,1)S(1)}, u32[]{:S(2)}, u32[]{:S(2)}) collective-permute-start(bf16[16,3072]{1,0:T(8,128)(2,1)} %bitcast.29), channel_id=1, source_target_pairs={{0,192},{4,60},{8,200},{12,4},{16,208},{20,12},{24,216},{28,20},{3... | collective-permute-start | bytes 294920 | tf_op jit(solution)/shard_map/ppermute | solution.py:31
  7.8 2.0 %collective-permute-done.1.refs_0_ = bf16[16,3072]{1,0:T(8,128)(2,1)S(1)} collective-permute-done((bf16[16,3072]{1,0:T(8,128)(2,1)}, bf16[16,3072]{1,0:T(8,128)(2,1)S(1)}, u32[]{:S(2)}, u32[]{:S(2)}) %collective-permute-start.1) | collective-permute-done | bytes 98336 | tf_op jit(solution)/shard_map/ppermute | solution.py:31
  9.8 2.9 %collective-permute-start.2 = (bf16[16,3072]{1,0:T(8,128)(2,1)S(1)}, bf16[16,3072]{1,0:T(8,128)(2,1)S(1)}, u32[]{:S(2)}, u32[]{:S(2)}) collective-permute-start(bf16[16,3072]{1,0:T(8,128)(2,1)S(1)} %collective-permute-done.1.refs_0_), channel_id=1, source_target_pairs={{0,192},{4,60},{8,200},{12,4},{16,208},{20,12},{24,216},{28,20},{3... | collective-permute-start | bytes 294920 | tf_op jit(solution)/shard_map/ppermute | solution.py:31
  14.4 1.3 %collective-permute-start.3 = (bf16[64,3072]{1,0:T(8,128)(2,1)S(1)}, bf16[64,3072]{1,0:T(8,128)(2,1)S(1)}, u32[]{:S(2)}, u32[]{:S(2)}) collective-permute-start(bf16[64,3072]{1,0:T(8,128)(2,1)S(1)} %shard_map.142.refs_0_), channel_id=1, source_target_pairs={{0,8},{4,68},{8,16},{12,76},{16,24},{20,84},{24,32},{28,92},{32,40... | collective-permute-start | bytes 1179656 | tf_op jit(solution)/shard_map/ppermute | solution.py:31
  15.7 1.9 %collective-permute-start.8 = (bf16[32,3072]{1,0:T(8,128)(2,1)S(1)}, bf16[32,3072]{1,0:T(8,128)(2,1)S(1)}, u32[]{:S(2)}, u32[]{:S(2)}) collective-permute-start(bf16[32,3072]{1,0:T(8,128)(2,1)S(1)} %shard_map.140.refs_0_), channel_id=1, source_target_pairs={{4,20},{12,28},{20,36},{28,44},{36,52},{44,60},{52,4},{60,12},{68,... | collective-permute-start | bytes 589832 | tf_op jit(solution)/shard_map/ppermute | solution.py:31
  17.6 5.5 %collective-permute-start.7 = (bf16[32,3072]{1,0:T(8,128)(2,1)S(1)}, bf16[32,3072]{1,0:T(8,128)(2,1)S(1)}, u32[]{:S(2)}, u32[]{:S(2)}) collective-permute-start(bf16[32,3072]{1,0:T(8,128)(2,1)S(1)} %shard_map.141.refs_1_), channel_id=1, source_target_pairs={{4,52},{12,60},{20,4},{28,12},{36,20},{44,28},{52,36},{60,44},{68,... | collective-permute-start | bytes 589832 | tf_op jit(solution)/shard_map/ppermute | solution.py:31
  23.2 1.6 %collective-permute-start.4 = (bf16[64,3072]{1,0:T(8,128)(2,1)S(1)}, bf16[64,3072]{1,0:T(8,128)(2,1)S(1)}, u32[]{:S(2)}, u32[]{:S(2)}) collective-permute-start(bf16[64,3072]{1,0:T(8,128)(2,1)S(1)} %shard_map.142.refs_0_), channel_id=1, source_target_pairs={{0,56},{4,196},{8,0},{12,204},{16,8},{20,212},{24,16},{28,220},{32... | collective-permute-start | bytes 1179656 | tf_op jit(solution)/shard_map/ppermute | solution.py:31
  24.8 3.0 %collective-permute-done.8.refs_1_ = bf16[32,3072]{1,0:T(8,128)(2,1)S(1)} collective-permute-done((bf16[32,3072]{1,0:T(8,128)(2,1)S(1)}, bf16[32,3072]{1,0:T(8,128)(2,1)S(1)}, u32[]{:S(2)}, u32[]{:S(2)}) %collective-permute-start.8) | collective-permute-done | bytes 196640 | tf_op jit(solution)/shard_map/ppermute | solution.py:31
  27.8 2.1 %collective-permute-done.7.refs_0_ = bf16[32,3072]{1,0:T(8,128)(2,1)S(1)} collective-permute-done((bf16[32,3072]{1,0:T(8,128)(2,1)S(1)}, bf16[32,3072]{1,0:T(8,128)(2,1)S(1)}, u32[]{:S(2)}, u32[]{:S(2)}) %collective-permute-start.7) | collective-permute-done | bytes 196640 | tf_op jit(solution)/shard_map/ppermute | solution.py:31
  30.4 1.3 %reduce.19 = s32[1024]{0:T(1024)S(1)} reduce(s32[1,1024]{1,0:T(1,128)} %param.14, s32[]{:T(128)} %broadcast.63), dimensions={0}, to_apply=%get-tuple-element.16.reduce_sub_computation.3 | reduce | bytes 8196 | tf_op jit(solution)/shard_map/optimization_barrier | solution.py:107
  33.9 6.0 %collective-permute-done.5.refs_3_.mine_ref = bf16[64,3072]{1,0:T(8,128)(2,1)S(1)} collective-permute-done((bf16[64,3072]{1,0:T(8,128)(2,1)S(1)}, bf16[64,3072]{1,0:T(8,128)(2,1)S(1)}, u32[]{:S(2)}, u32[]{:S(2)}) %collective-permute-start.5) | collective-permute-done | bytes 393248 | tf_op jit(solution)/shard_map/ppermute | solution.py:31
  40.1 2.7 %collective-permute-start.11 = (bf16[64,3072]{1,0:T(8,128)(2,1)S(1)}, bf16[64,3072]{1,0:T(8,128)(2,1)S(1)}, u32[]{:S(2)}, u32[]{:S(2)}) collective-permute-start(bf16[64,3072]{1,0:T(8,128)(2,1)S(1)} %shard_map.147), channel_id=1, source_target_pairs={{0,56},{4,196},{8,0},{12,204},{16,8},{20,212},{24,16},{28,220},{32... | collective-permute-start | bytes 1179656 | tf_op jit(solution)/shard_map/ppermute | solution.py:31
  42.8 5.3 %collective-permute-done.9.refs_0_ = bf16[64,3072]{1,0:T(8,128)(2,1)S(1)} collective-permute-done((bf16[64,3072]{1,0:T(8,128)(2,1)S(1)}, bf16[64,3072]{1,0:T(8,128)(2,1)S(1)}, u32[]{:S(2)}, u32[]{:S(2)}) %collective-permute-start.9) | collective-permute-done | bytes 393248 | tf_op jit(solution)/shard_map/ppermute | solution.py:31
  48.2 6.4 %shard_map.143.refs_6_ = f32[8,256]{1,0:T(8,128)S(1)} custom-call(bf16[64,3072]{1,0:T(8,128)(2,1)S(1)} %shard_map.142.refs_0_, bf16[64,3072]{1,0:T(8,128)(2,1)S(1)} %collective-permute-done.3.refs_1_, bf16[64,3072]{1,0:T(8,128)(2,1)S(1)} %collective-permute-done.4.refs_2_, bf16[64,3072]{1,0:T(8,128)(2,1)S(1)} %collective-permute-done.5.refs_3_.mine_ref, ...), custom_call_target="tpu_custom_call" | custom-call | flops 3221225472 | bytes 12582912 | tf_op jit(solution)/shard_map/pallas_call | solution.py:184
  54.6 6.5 %shard_map.144 = f32[8,256]{1,0:T(8,128)S(1)} custom-call(bf16[64,3072]{1,0:T(8,128)(2,1)S(1)} %shard_map.142.refs_0_, bf16[64,3072]{1,0:T(8,128)(2,1)S(1)} %collective-permute-done.3.refs_1_, bf16[64,3072]{1,0:T(8,128)(2,1)S(1)} %collective-permute-done.4.refs_2_, bf16[64,3072]{1,0:T(8,128)(2,1)S(1)} %collective-permute-done.5.refs_3_.mine_ref, ...), custom_call_target="tpu_custom_call" | custom-call | flops 3221225472 | bytes 12582912 | tf_op jit(solution)/shard_map/pallas_call | solution.py:184
  61.2 11.0 %shard_map.148 = f32[8,256]{1,0:T(8,128)S(1)} custom-call(bf16[64,3072]{1,0:T(8,128)(2,1)S(1)} %collective-permute-done.9.refs_0_, bf16[64,3072]{1,0:T(8,128)(2,1)S(1)} %collective-permute-done.11.refs_1_, bf16[64,3072]{1,0:T(8,128)(2,1)S(1)} %collective-permute-done.12.refs_2_, bf16[64,3072]{1,0:T(8,128)(2,1)S(1)} %collective-permute-done.10.mine_ref.refs_3_, ...), custom_call_target="tpu_custom_call" | custom-call | flops 6442450944 | bytes 25165824 | tf_op jit(solution)/shard_map/pallas_call | solution.py:184
  73.9 7.8 %all-to-all-start = ((f32[32,3,512]{2,1,0:T(4,128)}), f32[32,3,512]{2,1,0:T(4,128)S(1)}, u32[]{:S(2)}, u32[]{:S(2)}) async-start(f32[32,3,512]{2,1,0:T(4,128)} %broadcast_in_dim.44), calls=%async_computation | async-start | bytes 524288 | tf_op jit(solution)/shard_map/all_to_all | solution.py:252
  82.3 8.9 %all-to-all-done = f32[32,3,512]{2,1,0:T(4,128)S(1)} async-done(((f32[32,3,512]{2,1,0:T(4,128)}), f32[32,3,512]{2,1,0:T(4,128)S(1)}, u32[]{:S(2)}, u32[]{:S(2)}) %all-to-all-start) | async-done | bytes 196640 | tf_op jit(solution)/shard_map/all_to_all | solution.py:252
  91.6 3.8 %collective-permute-start.13 = (f32[16]{0:T(128)S(1)}, f32[16]{0:T(128)S(1)}, u32[]{:S(2)}, u32[]{:S(2)}) collective-permute-start(f32[16]{0:T(128)S(1)} %multiply_reduce_fusion), channel_id=1, source_target_pairs={{0,4},{4,0},{8,12},{12,8},{16,20},{20,16},{24,28},{28,24},{32,36},... | collective-permute-start | bytes 200 | tf_op jit(solution)/shard_map/ppermute | solution.py:36
  96.2 1.3 %collective-permute-start.14 = (f32[16]{0:T(128)S(1)}, f32[16]{0:T(128)S(1)}, u32[]{:S(2)}, u32[]{:S(2)}) collective-permute-start(f32[16]{0:T(128)S(1)} %add.69), channel_id=1, source_target_pairs={{0,1},{1,2},{2,3},{3,0},{4,5},{5,6},{6,7},{7,4},{8,9},{9,10},{10,1... | collective-permute-start | bytes 200 | tf_op jit(solution)/shard_map/ppermute | solution.py:266
  97.5 1.4 %collective-permute-start.15 = (f32[16]{0:T(128)S(1)}, f32[16]{0:T(128)S(1)}, u32[]{:S(2)}, u32[]{:S(2)}) collective-permute-start(f32[16]{0:T(128)S(1)} %add.69), channel_id=1, source_target_pairs={{0,3},{1,0},{2,1},{3,2},{4,7},{5,4},{6,5},{7,6},{8,11},{9,8},{10,9... | collective-permute-start | bytes 200 | tf_op jit(solution)/shard_map/ppermute | solution.py:266
  98.9 1.6 %collective-permute-start.16 = (f32[16]{0:T(128)S(1)}, f32[16]{0:T(128)S(1)}, u32[]{:S(2)}, u32[]{:S(2)}) collective-permute-start(f32[16]{0:T(128)S(1)} %add.69), channel_id=1, source_target_pairs={{0,2},{1,3},{2,0},{3,1},{4,6},{5,7},{6,4},{7,5},{8,10},{9,11},{10,... | collective-permute-start | bytes 200 | tf_op jit(solution)/shard_map/ppermute | solution.py:266
  100.6 2.3 %collective-permute-done.16 = f32[16]{0:T(128)S(1)} collective-permute-done((f32[16]{0:T(128)S(1)}, f32[16]{0:T(128)S(1)}, u32[]{:S(2)}, u32[]{:S(2)}) %collective-permute-start.16) | collective-permute-done | bytes 96 | tf_op jit(solution)/shard_map/ppermute | solution.py:266
  (67 shorter events, 9.2 us)
Async XLA Ops:
  0.6 81.6 %copy-start = (s32[1,4]{1,0:T(1,128)S(1)}, s32[1,4]{1,0:T(1,128)}, u32[]{:S(2)}) copy-start(s32[1,4]{1,0:T(1,128)} %param.16) | copy-start | bytes 52
  0.6 54.0 %collective-permute-start.6 = (bf16[2048,3072]{1,0:T(8,128)(2,1)}, bf16[2048,3072]{1,0:T(8,128)(2,1)}, u32[]{:S(2)}, u32[]{:S(2)}) collective-permute-start(bf16[2048,3072]{1,0:T(8,128)(2,1)} %refs_6_.1), channel_id=1, source_target_pairs={{0,4},{4,0},{8,12},{12,8},{16,20},{20,16},{24,28},{28,24},{32,36},... | collective-permute-start | bytes 37748744 | tf_op jit(solution)/shard_map/ppermute | solution.py:36
  3.9 5.8 %collective-permute-start.1 = (bf16[16,3072]{1,0:T(8,128)(2,1)}, bf16[16,3072]{1,0:T(8,128)(2,1)S(1)}, u32[]{:S(2)}, u32[]{:S(2)}) collective-permute-start(bf16[16,3072]{1,0:T(8,128)(2,1)} %bitcast.29), channel_id=1, source_target_pairs={{0,192},{4,60},{8,200},{12,4},{16,208},{20,12},{24,216},{28,20},{3... | collective-permute-start | bytes 294920 | tf_op jit(solution)/shard_map/ppermute | solution.py:31
  7.8 5.8 %collective-permute-start = (bf16[16,3072]{1,0:T(8,128)(2,1)}, bf16[16,3072]{1,0:T(8,128)(2,1)S(1)}, u32[]{:S(2)}, u32[]{:S(2)}) collective-permute-start(bf16[16,3072]{1,0:T(8,128)(2,1)} %bitcast.30), channel_id=1, source_target_pairs={{0,64},{4,12},{8,72},{12,20},{16,80},{20,28},{24,88},{28,36},{32,9... | collective-permute-start | bytes 294920 | tf_op jit(solution)/shard_map/ppermute | solution.py:31
  9.8 4.6 %collective-permute-start.2 = (bf16[16,3072]{1,0:T(8,128)(2,1)S(1)}, bf16[16,3072]{1,0:T(8,128)(2,1)S(1)}, u32[]{:S(2)}, u32[]{:S(2)}) collective-permute-start(bf16[16,3072]{1,0:T(8,128)(2,1)S(1)} %collective-permute-done.1.refs_0_), channel_id=1, source_target_pairs={{0,192},{4,60},{8,200},{12,4},{16,208},{20,12},{24,216},{28,20},{3... | collective-permute-start | bytes 294920 | tf_op jit(solution)/shard_map/ppermute | solution.py:31
  12.7 0.9 copy-start.1
  14.4 15.5 %collective-permute-start.3 = (bf16[64,3072]{1,0:T(8,128)(2,1)S(1)}, bf16[64,3072]{1,0:T(8,128)(2,1)S(1)}, u32[]{:S(2)}, u32[]{:S(2)}) collective-permute-start(bf16[64,3072]{1,0:T(8,128)(2,1)S(1)} %shard_map.142.refs_0_), channel_id=1, source_target_pairs={{0,8},{4,68},{8,16},{12,76},{16,24},{20,84},{24,32},{28,92},{32,40... | collective-permute-start | bytes 1179656 | tf_op jit(solution)/shard_map/ppermute | solution.py:31
  15.7 12.1 %collective-permute-start.8 = (bf16[32,3072]{1,0:T(8,128)(2,1)S(1)}, bf16[32,3072]{1,0:T(8,128)(2,1)S(1)}, u32[]{:S(2)}, u32[]{:S(2)}) collective-permute-start(bf16[32,3072]{1,0:T(8,128)(2,1)S(1)} %shard_map.140.refs_0_), channel_id=1, source_target_pairs={{4,20},{12,28},{20,36},{28,44},{36,52},{44,60},{52,4},{60,12},{68,... | collective-permute-start | bytes 589832 | tf_op jit(solution)/shard_map/ppermute | solution.py:31
  17.6 12.3 %collective-permute-start.7 = (bf16[32,3072]{1,0:T(8,128)(2,1)S(1)}, bf16[32,3072]{1,0:T(8,128)(2,1)S(1)}, u32[]{:S(2)}, u32[]{:S(2)}) collective-permute-start(bf16[32,3072]{1,0:T(8,128)(2,1)S(1)} %shard_map.141.refs_1_), channel_id=1, source_target_pairs={{4,52},{12,60},{20,4},{28,12},{36,20},{44,28},{52,36},{60,44},{68,... | collective-permute-start | bytes 589832 | tf_op jit(solution)/shard_map/ppermute | solution.py:31
  23.2 9.9 %collective-permute-start.4 = (bf16[64,3072]{1,0:T(8,128)(2,1)S(1)}, bf16[64,3072]{1,0:T(8,128)(2,1)S(1)}, u32[]{:S(2)}, u32[]{:S(2)}) collective-permute-start(bf16[64,3072]{1,0:T(8,128)(2,1)S(1)} %shard_map.142.refs_0_), channel_id=1, source_target_pairs={{0,56},{4,196},{8,0},{12,204},{16,8},{20,212},{24,16},{28,220},{32... | collective-permute-start | bytes 1179656 | tf_op jit(solution)/shard_map/ppermute | solution.py:31
  31.9 8.0 %collective-permute-start.5 = (bf16[64,3072]{1,0:T(8,128)(2,1)S(1)}, bf16[64,3072]{1,0:T(8,128)(2,1)S(1)}, u32[]{:S(2)}, u32[]{:S(2)}) collective-permute-start(bf16[64,3072]{1,0:T(8,128)(2,1)S(1)} %collective-permute-done.3.refs_1_), channel_id=1, source_target_pairs={{0,8},{4,68},{8,16},{12,76},{16,24},{20,84},{24,32},{28,92},{32,40... | collective-permute-start | bytes 1179656 | tf_op jit(solution)/shard_map/ppermute | solution.py:31
  33.1 6.9 %collective-permute-start.10 = (bf16[64,3072]{1,0:T(8,128)(2,1)S(1)}, bf16[64,3072]{1,0:T(8,128)(2,1)S(1)}, u32[]{:S(2)}, u32[]{:S(2)}) collective-permute-start(bf16[64,3072]{1,0:T(8,128)(2,1)S(1)} %collective-permute-done.4.refs_2_), channel_id=1, source_target_pairs={{0,56},{8,0},{16,8},{24,16},{32,24},{40,32},{48,40},{56,48},{64,12... | collective-permute-start | bytes 1179656 | tf_op jit(solution)/shard_map/ppermute | solution.py:31
  40.0 8.2 %collective-permute-start.9 = (bf16[64,3072]{1,0:T(8,128)(2,1)S(1)}, bf16[64,3072]{1,0:T(8,128)(2,1)S(1)}, u32[]{:S(2)}, u32[]{:S(2)}) collective-permute-start(bf16[64,3072]{1,0:T(8,128)(2,1)S(1)} %shard_map.146), channel_id=1, source_target_pairs={{0,8},{4,68},{8,16},{12,76},{16,24},{20,84},{24,32},{28,92},{32,40... | collective-permute-start | bytes 1179656 | tf_op jit(solution)/shard_map/ppermute | solution.py:31
  40.1 21.0 %collective-permute-start.11 = (bf16[64,3072]{1,0:T(8,128)(2,1)S(1)}, bf16[64,3072]{1,0:T(8,128)(2,1)S(1)}, u32[]{:S(2)}, u32[]{:S(2)}) collective-permute-start(bf16[64,3072]{1,0:T(8,128)(2,1)S(1)} %shard_map.147), channel_id=1, source_target_pairs={{0,56},{4,196},{8,0},{12,204},{16,8},{20,212},{24,16},{28,220},{32... | collective-permute-start | bytes 1179656 | tf_op jit(solution)/shard_map/ppermute | solution.py:31
  48.2 13.0 %collective-permute-start.12 = (bf16[64,3072]{1,0:T(8,128)(2,1)S(1)}, bf16[64,3072]{1,0:T(8,128)(2,1)S(1)}, u32[]{:S(2)}, u32[]{:S(2)}) collective-permute-start(bf16[64,3072]{1,0:T(8,128)(2,1)S(1)} %collective-permute-done.9.refs_0_), channel_id=1, source_target_pairs={{0,8},{4,68},{8,16},{12,76},{16,24},{20,84},{24,32},{28,92},{32,40... | collective-permute-start | bytes 1179656 | tf_op jit(solution)/shard_map/ppermute | solution.py:31
  61.1 11.6 %copy-start.2 = (s32[1,1024]{1,0:T(1,128)S(1)}, s32[1,1024]{1,0:T(1,128)}, u32[]{:S(2)}) copy-start(s32[1,1024]{1,0:T(1,128)} %param.15) | copy-start | bytes 12292
  61.1 20.7 %copy-start.3 = (f32[16]{0:T(128)S(1)}, f32[16]{0:T(128)}, u32[]{:S(2)}) copy-start(f32[16]{0:T(128)} %param.17) | copy-start | bytes 196
  73.9 17.3 %all-to-all-start = ((f32[32,3,512]{2,1,0:T(4,128)}), f32[32,3,512]{2,1,0:T(4,128)S(1)}, u32[]{:S(2)}, u32[]{:S(2)}) async-start(f32[32,3,512]{2,1,0:T(4,128)} %broadcast_in_dim.44), calls=%async_computation | async-start | bytes 524288 | tf_op jit(solution)/shard_map/all_to_all | solution.py:252
  91.6 4.6 %collective-permute-start.13 = (f32[16]{0:T(128)S(1)}, f32[16]{0:T(128)S(1)}, u32[]{:S(2)}, u32[]{:S(2)}) collective-permute-start(f32[16]{0:T(128)S(1)} %multiply_reduce_fusion), channel_id=1, source_target_pairs={{0,4},{4,0},{8,12},{12,8},{16,20},{20,16},{24,28},{28,24},{32,36},... | collective-permute-start | bytes 200 | tf_op jit(solution)/shard_map/ppermute | solution.py:36
  96.2 4.4 %collective-permute-start.14 = (f32[16]{0:T(128)S(1)}, f32[16]{0:T(128)S(1)}, u32[]{:S(2)}, u32[]{:S(2)}) collective-permute-start(f32[16]{0:T(128)S(1)} %add.69), channel_id=1, source_target_pairs={{0,1},{1,2},{2,3},{3,0},{4,5},{5,6},{6,7},{7,4},{8,9},{9,10},{10,1... | collective-permute-start | bytes 200 | tf_op jit(solution)/shard_map/ppermute | solution.py:266
  97.5 3.1 %collective-permute-start.15 = (f32[16]{0:T(128)S(1)}, f32[16]{0:T(128)S(1)}, u32[]{:S(2)}, u32[]{:S(2)}) collective-permute-start(f32[16]{0:T(128)S(1)} %add.69), channel_id=1, source_target_pairs={{0,3},{1,0},{2,1},{3,2},{4,7},{5,4},{6,5},{7,6},{8,11},{9,8},{10,9... | collective-permute-start | bytes 200 | tf_op jit(solution)/shard_map/ppermute | solution.py:266
  98.9 3.9 %collective-permute-start.16 = (f32[16]{0:T(128)S(1)}, f32[16]{0:T(128)S(1)}, u32[]{:S(2)}, u32[]{:S(2)}) collective-permute-start(f32[16]{0:T(128)S(1)} %add.69), channel_id=1, source_target_pairs={{0,2},{1,3},{2,0},{3,1},{4,6},{5,7},{6,4},{7,5},{8,10},{9,11},{10,... | collective-permute-start | bytes 200 | tf_op jit(solution)/shard_map/ppermute | solution.py:266

commit v2 on v1

--- a/solution.py
+++ b/solution.py
@@ -91,7 +91,7 @@
     out_ref[...] = in_ref[...]
 
 
-def gather_quads(own, first, *small):
+def gather_quads(own, first):
     kept = pl.pallas_call(
         copy_kernel, in_specs=[VMEM], out_specs=VMEM, out_shape=pltpu.VMEM(own.shape, own.dtype), compiler_params=SMALL
     )(own)
@@ -104,17 +104,16 @@
     q1m = move(q0, (ZM, XM))
     f3 = move(ahead, (None, (0, -2)))
     f5 = move(behind, (None, (0, 2)))
-    q1p, *small = lax.optimization_barrier((q1p, *small))
     q2p = move(q1p, (ZP, XP))
     q2m = move(q1m, (ZM, None))
     far = join(f3, f5)
     q3p = move(pick(first, q2p, far), (ZP, XP))
     q3m = move(pick(first, q2m, far), (ZM, XM))
     q4 = move(q3p, (ZP, XP))
-    return (q0, q1p, q1m, q2p, q3p, q3m, q4, q2m, far), small
-
-
-def stats_kernel(*refs, pieces, heads, seeded):
+    return q0, q1p, q1m, q2p, q3p, q3m, q4, q2m, far
+
+
+def stats_kernel(*refs, pieces, heads, seeded, chunk, first_head):
     x_refs = refs[:pieces]
     target_ref = refs[pieces]
     head_refs = refs[pieces + 1 : pieces + 1 + heads]
@@ -159,7 +158,7 @@
         tiles_ref[slot], rows_ref[...], (((1,), (1,)), ((), ())), preferred_element_type=jnp.float32
     )
     which = step // per_head
-    target = target_ref[0:1, :] if heads == 1 else jnp.where(which == 0, target_ref[0:1, :], target_ref[1:2, :])
+    target = target_ref[chunk, pl.ds(first_head + which, 1), :]
     old_max = out_ref[0:1, :]
     new_max = jnp.maximum(old_max, jnp.max(logits, axis=0, keepdims=True))
     index = lax.broadcasted_iota(jnp.int32, logits.shape, 0)
@@ -171,9 +170,9 @@
     out_ref[0:1, :] = new_max
 
 
-def chunk_stats(xs, targets, heads, seed=None):
+def chunk_stats(xs, targets, chunk, first_head, heads, seed=None):
     vocab_rows, width = heads[0].shape
-    rows = targets.shape[1]
+    rows = targets.shape[2]
     ins = [*held(*xs), targets, *(pltpu.with_memory_space_constraint(h, pltpu.HBM) for h in heads)]
     whole = lambda a: pl.BlockSpec(a.shape, lambda i: (0,) * a.ndim)
     specs = [VMEM for x in xs] + [whole(targets)] + [pl.BlockSpec(memory_space=pltpu.HBM) for h in heads]
@@ -182,7 +181,14 @@
         specs.append(whole(seed))
     work = len(heads) * vocab_rows
     return pl.pallas_call(
-        functools.partial(stats_kernel, pieces=len(xs), heads=len(heads), seeded=seed is not None),
+        functools.partial(
+            stats_kernel,
+            pieces=len(xs),
+            heads=len(heads),
+            seeded=seed is not None,
+            chunk=chunk,
+            first_head=first_head,
+        ),
         grid=(work // TILE,),
         in_specs=specs,
         out_specs=pl.BlockSpec((8, rows), lambda i: (0, 0)),
@@ -220,8 +226,7 @@
 
     other_head = swap_cores(head)
     flag = jnp.reshape(1 - core, (1,))
-    quads, (labels, s, z, core) = gather_quads(hidden[0], flag, labels, s, z, core)
-    first = core == 0
+    quads = gather_quads(hidden[0], flag)
     early, late = quads[:4], quads[4:]
 
     n = np.arange(8 * 4 * rows)
@@ -237,9 +242,9 @@
     target = jnp.sum(jnp.where(hit, lab[:, None], 0), axis=0).reshape(2, 1, 4 * 4 * rows)
     target = target - jnp.stack([position, position ^ 1])[None, :, None] * vocab_rows
 
-    stats1 = chunk_stats(early, target[0, :1], [head])
-    stats1 = chunk_stats(early, target[0, 1:], [other_head], stats1)
-    stats2 = chunk_stats(late, target[1], [head, other_head])
+    stats1 = chunk_stats(early, target, 0, 0, [head])
+    stats1 = chunk_stats(early, target, 0, 1, [other_head], stats1)
+    stats2 = chunk_stats(late, target, 1, 0, [head, other_head])
 
     stats = jnp.concatenate([stats1, stats2], axis=1)
     stats = lax.dot_general(
@@ -247,25 +252,26 @@
     )[:3]
 
     same_core = [[NC * k + c for k in range(NS * NZ)] for c in range(NC)]
-    stats, response_mask, seq_pair, ref_logp = lax.optimization_barrier((stats, response_mask, seq_pair, ref_logp))
     sent = copies(stats, NS * NZ)
     pieces = lax.all_to_all(sent, PLANE, split_axis=0, concat_axis=0, tiled=True, axis_index_groups=same_core)
     top, total, label_logit = combine(pieces)
     logprob = label_logit - top - jnp.log(total)
-    token_logprob = lax.dynamic_slice_in_dim(logprob, (s * NZ + z) * rows, rows)[None, :]
 
     slot_count = ref_logp.shape[0]
+    ref_gap = ref_logp[0::2] - ref_logp[1::2]
+    own_start = (s * NZ + z) * rows
     weights = response_mask[0].astype(jnp.float32).reshape(NS, NZ * NC * rows)
     weights = weights / jnp.sum(weights, axis=1, keepdims=True)
     weights = mine(weights.reshape(NS * NZ, NC, rows))
     slots = jnp.broadcast_to(seq_pair[0][:, None], (NS, NZ * rows)).reshape(-1)
     slot_ids = lax.broadcasted_iota(jnp.int32, (slot_count, slots.shape[0]), 0)
     by_slot = jnp.where(slots[None, :] == slot_ids, weights[None, :], 0.0)
+    token_logprob = lax.dynamic_slice_in_dim(logprob, own_start, rows, allow_negative_indices=False)[None, :]
     part = jnp.sum(by_slot * logprob[None, :], axis=1)
     part = part + swap_cores(part)
     around = [lax.ppermute(part, "dp", [(i, (i + d) % 4) for i in range(4)]) for d in (1, 3, 2)]
     policy = part + around[0] + around[1] + around[2]
-    pair_margin = beta_scale * (policy[0::2] - ref_logp[0::2] - (policy[1::2] - ref_logp[1::2]))
+    pair_margin = beta_scale * (policy[0::2] - policy[1::2] - ref_gap)
     loss = jnp.mean(jnp.logaddexp(0.0, -pair_margin))
     return (token_logprob, pair_margin, loss)
 

time: 107 us -> 104 us (0.972)
  waiting for transfers between devices: 30.6 us -> 25.5 us
  other arithmetic: 4.31 us -> 5.67 us
  starting transfers between devices: 40 us -> 41.1 us
    ppermute x12, waiting for transfers between devices: 19.1 us -> 14 us  [move(): return lax.ppermute(x, PLANE, pairs)]
    convert_element_type x2, other arithmetic: 0.03 us -> 1.39 us  [step(): weights = response_mask[0].astype(jnp.float32).reshape(NS, NZ * NC * rows)]
    optimization_barrier x1 -> x0, other arithmetic: 1.35 us -> none  [gather_quads(): q1p, *small = lax.optimization_barrier((q1p, *small))]
    unnamed x0 -> x1, other arithmetic: none -> 1.35 us
  transfers between devices with their start and end apart: 18 -> 18, of which waited for: 9 -> 9; matrix products, arithmetic and copies ran while one was open for 4% -> 6% of each run, Pallas kernels for 12% -> 13%
where the time goes in v2:
time: 104 us; the launch traced here: 103 us
  starting transfers between devices  41.1 us (40%)
  waiting for transfers between devices  25.5 us (25%)
  Pallas kernels  24.1 us (23%)
  other arithmetic  5.67 us (5%)
  local copies, waits for them, and re-layouts  3.73 us (4%)
  between operations  2.67 us (3%)
    pallas_call x3, Pallas kernels, chunk_stats(): pl.pallas_call(functools.partial(stats_kernel, pieces=len(xs), heads=len(...  23.9 us
    ppermute x12, starting transfers between devices, move(): return lax.ppermute(x, PLANE, pairs)  21 us
    ppermute x12, waiting for transfers between devices, move(): return lax.ppermute(x, PLANE, pairs)  14 us
    all_to_all x1, waiting for transfers between devices, step(): lax.all_to_all(sent, PLANE, split_axis=0, concat_axis=0, tiled=True, axis...  8.93 us
    all_to_all x1, starting transfers between devices, step(): lax.all_to_all(sent, PLANE, split_axis=0, concat_axis=0, tiled=True, axis...  8.66 us
    ppermute x2, starting transfers between devices, swap_cores(): return lax.ppermute(x, PLANE, pairs)  7.05 us
    ppermute x3, starting transfers between devices, step(): lax.ppermute(part, 'dp', [(i, (i + d) % 4) for i in range(4)])  4.39 us
    ppermute x3, waiting for transfers between devices, step(): lax.ppermute(part, 'dp', [(i, (i + d) % 4) for i in range(4)])  2.28 us
  transfers between devices with their start and end apart: 18, of which 9 were waited for; matrix products, arithmetic and copies ran while one was open for 6% of the time, Pallas kernels for 13%

profile of v2, /device:TPU:1, one launch (start us, length us, event | category | flops | bytes accessed | tf_op | source)
XLA Modules:
  0.0 103.3 jit_solution(6669078421293237103)
XLA Ops:
  0.6 3.3 %collective-permute-start.6 = (bf16[2048,3072]{1,0:T(8,128)(2,1)}, bf16[2048,3072]{1,0:T(8,128)(2,1)}, u32[]{:S(2)}, u32[]{:S(2)}) collective-permute-start(bf16[2048,3072]{1,0:T(8,128)(2,1)} %refs_6_.1), channel_id=1, source_target_pairs={{0,4},{4,0},{8,12},{12,8},{16,20},{20,16},{24,28},{28,24},{32,36},... | collective-permute-start | bytes 37748744 | tf_op jit(solution)/shard_map/ppermute | solution.py:36
  3.9 3.9 %collective-permute-start.1 = (bf16[16,3072]{1,0:T(8,128)(2,1)}, bf16[16,3072]{1,0:T(8,128)(2,1)S(1)}, u32[]{:S(2)}, u32[]{:S(2)}) collective-permute-start(bf16[16,3072]{1,0:T(8,128)(2,1)} %bitcast.23), channel_id=1, source_target_pairs={{0,192},{4,60},{8,200},{12,4},{16,208},{20,12},{24,216},{28,20},{3... | collective-permute-start | bytes 294920 | tf_op jit(solution)/shard_map/ppermute | solution.py:31
  7.8 2.0 %collective-permute-done.1.refs_0_ = bf16[16,3072]{1,0:T(8,128)(2,1)S(1)} collective-permute-done((bf16[16,3072]{1,0:T(8,128)(2,1)}, bf16[16,3072]{1,0:T(8,128)(2,1)S(1)}, u32[]{:S(2)}, u32[]{:S(2)}) %collective-permute-start.1) | collective-permute-done | bytes 98336 | tf_op jit(solution)/shard_map/ppermute | solution.py:31
  9.8 2.9 %collective-permute-start.2 = (bf16[16,3072]{1,0:T(8,128)(2,1)S(1)}, bf16[16,3072]{1,0:T(8,128)(2,1)S(1)}, u32[]{:S(2)}, u32[]{:S(2)}) collective-permute-start(bf16[16,3072]{1,0:T(8,128)(2,1)S(1)} %collective-permute-done.1.refs_0_), channel_id=1, source_target_pairs={{0,192},{4,60},{8,200},{12,4},{16,208},{20,12},{24,216},{28,20},{3... | collective-permute-start | bytes 294920 | tf_op jit(solution)/shard_map/ppermute | solution.py:31
  14.4 1.3 %collective-permute-start.3 = (bf16[64,3072]{1,0:T(8,128)(2,1)S(1)}, bf16[64,3072]{1,0:T(8,128)(2,1)S(1)}, u32[]{:S(2)}, u32[]{:S(2)}) collective-permute-start(bf16[64,3072]{1,0:T(8,128)(2,1)S(1)} %shard_map.142.refs_0_), channel_id=1, source_target_pairs={{0,8},{4,68},{8,16},{12,76},{16,24},{20,84},{24,32},{28,92},{32,40... | collective-permute-start | bytes 1179656 | tf_op jit(solution)/shard_map/ppermute | solution.py:31
  16.2 1.3 %reduce.19 = s32[1024]{0:T(1024)S(1)} reduce(s32[1,1024]{1,0:T(1,128)} %param.14, s32[]{:T(128)} %broadcast.63), dimensions={0}, to_apply=%param.14.reduce_sub_computation.3 | reduce | bytes 8196 | tf_op args[2]
  17.7 1.7 %collective-permute-start.4 = (bf16[64,3072]{1,0:T(8,128)(2,1)S(1)}, bf16[64,3072]{1,0:T(8,128)(2,1)S(1)}, u32[]{:S(2)}, u32[]{:S(2)}) collective-permute-start(bf16[64,3072]{1,0:T(8,128)(2,1)S(1)} %shard_map.142.refs_0_), channel_id=1, source_target_pairs={{0,56},{4,196},{8,0},{12,204},{16,8},{20,212},{24,16},{28,220},{32... | collective-permute-start | bytes 1179656 | tf_op jit(solution)/shard_map/ppermute | solution.py:31
  19.3 3.4 %collective-permute-done.3.refs_1_ = bf16[64,3072]{1,0:T(8,128)(2,1)S(1)} collective-permute-done((bf16[64,3072]{1,0:T(8,128)(2,1)S(1)}, bf16[64,3072]{1,0:T(8,128)(2,1)S(1)}, u32[]{:S(2)}, u32[]{:S(2)}) %collective-permute-start.3) | collective-permute-done | bytes 393248 | tf_op jit(solution)/shard_map/ppermute | solution.py:31
  23.4 1.9 %collective-permute-start.8 = (bf16[32,3072]{1,0:T(8,128)(2,1)S(1)}, bf16[32,3072]{1,0:T(8,128)(2,1)S(1)}, u32[]{:S(2)}, u32[]{:S(2)}) collective-permute-start(bf16[32,3072]{1,0:T(8,128)(2,1)S(1)} %shard_map.140.refs_0_), channel_id=1, source_target_pairs={{4,20},{12,28},{20,36},{28,44},{36,52},{44,60},{52,4},{60,12},{68,... | collective-permute-start | bytes 589832 | tf_op jit(solution)/shard_map/ppermute | solution.py:31
  25.4 5.5 %collective-permute-start.7 = (bf16[32,3072]{1,0:T(8,128)(2,1)S(1)}, bf16[32,3072]{1,0:T(8,128)(2,1)S(1)}, u32[]{:S(2)}, u32[]{:S(2)}) collective-permute-start(bf16[32,3072]{1,0:T(8,128)(2,1)S(1)} %shard_map.141.refs_1_), channel_id=1, source_target_pairs={{4,52},{12,60},{20,4},{28,12},{36,20},{44,28},{52,36},{60,44},{68,... | collective-permute-start | bytes 589832 | tf_op jit(solution)/shard_map/ppermute | solution.py:31
  31.9 3.8 %collective-permute-done.8.refs_1_ = bf16[32,3072]{1,0:T(8,128)(2,1)S(1)} collective-permute-done((bf16[32,3072]{1,0:T(8,128)(2,1)S(1)}, bf16[32,3072]{1,0:T(8,128)(2,1)S(1)}, u32[]{:S(2)}, u32[]{:S(2)}) %collective-permute-start.8) | collective-permute-done | bytes 196640 | tf_op jit(solution)/shard_map/ppermute | solution.py:31
  36.6 1.6 %collective-permute-start.9 = (bf16[64,3072]{1,0:T(8,128)(2,1)S(1)}, bf16[64,3072]{1,0:T(8,128)(2,1)S(1)}, u32[]{:S(2)}, u32[]{:S(2)}) collective-permute-start(bf16[64,3072]{1,0:T(8,128)(2,1)S(1)} %shard_map.146), channel_id=1, source_target_pairs={{0,8},{4,68},{8,16},{12,76},{16,24},{20,84},{24,32},{28,92},{32,40... | collective-permute-start | bytes 1179656 | tf_op jit(solution)/shard_map/ppermute | solution.py:31
  39.5 1.5 %collective-permute-start.11 = (bf16[64,3072]{1,0:T(8,128)(2,1)S(1)}, bf16[64,3072]{1,0:T(8,128)(2,1)S(1)}, u32[]{:S(2)}, u32[]{:S(2)}) collective-permute-start(bf16[64,3072]{1,0:T(8,128)(2,1)S(1)} %shard_map.147), channel_id=1, source_target_pairs={{0,56},{4,196},{8,0},{12,204},{16,8},{20,212},{24,16},{28,220},{32... | collective-permute-start | bytes 1179656 | tf_op jit(solution)/shard_map/ppermute | solution.py:31
  40.9 4.1 %collective-permute-done.9.refs_0_ = bf16[64,3072]{1,0:T(8,128)(2,1)S(1)} collective-permute-done((bf16[64,3072]{1,0:T(8,128)(2,1)S(1)}, bf16[64,3072]{1,0:T(8,128)(2,1)S(1)}, u32[]{:S(2)}, u32[]{:S(2)}) %collective-permute-start.9) | collective-permute-done | bytes 393248 | tf_op jit(solution)/shard_map/ppermute | solution.py:31
  45.1 6.4 %shard_map.143.refs_6_ = f32[8,256]{1,0:T(8,128)S(1)} custom-call(bf16[64,3072]{1,0:T(8,128)(2,1)S(1)} %shard_map.142.refs_0_, bf16[64,3072]{1,0:T(8,128)(2,1)S(1)} %collective-permute-done.3.refs_1_, bf16[64,3072]{1,0:T(8,128)(2,1)S(1)} %collective-permute-done.4.refs_2_, bf16[64,3072]{1,0:T(8,128)(2,1)S(1)} %collective-permute-done.5.refs_3_.mine_ref, ...), custom_call_target="tpu_custom_call" | custom-call | flops 3221225472 | bytes 12582912 | tf_op jit(solution)/shard_map/pallas_call | solution.py:183
  51.6 6.5 %shard_map.144 = f32[8,256]{1,0:T(8,128)S(1)} custom-call(bf16[64,3072]{1,0:T(8,128)(2,1)S(1)} %shard_map.142.refs_0_, bf16[64,3072]{1,0:T(8,128)(2,1)S(1)} %collective-permute-done.3.refs_1_, bf16[64,3072]{1,0:T(8,128)(2,1)S(1)} %collective-permute-done.4.refs_2_, bf16[64,3072]{1,0:T(8,128)(2,1)S(1)} %collective-permute-done.5.refs_3_.mine_ref, ...), custom_call_target="tpu_custom_call" | custom-call | flops 3221225472 | bytes 12582912 | tf_op jit(solution)/shard_map/pallas_call | solution.py:183
  58.1 11.0 %shard_map.148 = f32[8,256]{1,0:T(8,128)S(1)} custom-call(bf16[64,3072]{1,0:T(8,128)(2,1)S(1)} %collective-permute-done.9.refs_0_, bf16[64,3072]{1,0:T(8,128)(2,1)S(1)} %collective-permute-done.11.refs_1_, bf16[64,3072]{1,0:T(8,128)(2,1)S(1)} %collective-permute-done.12.refs_2_, bf16[64,3072]{1,0:T(8,128)(2,1)S(1)} %collective-permute-done.10.mine_ref.refs_3_, ...), custom_call_target="tpu_custom_call" | custom-call | flops 6442450944 | bytes 25165824 | tf_op jit(solution)/shard_map/pallas_call | solution.py:183
  70.4 8.7 %all-to-all-start = ((f32[32,3,512]{2,1,0:T(4,128)}), f32[32,3,512]{2,1,0:T(4,128)S(1)}, u32[]{:S(2)}, u32[]{:S(2)}) async-start(f32[32,3,512]{2,1,0:T(4,128)} %broadcast_in_dim.44), calls=%async_computation | async-start | bytes 524288 | tf_op jit(solution)/shard_map/all_to_all | solution.py:256
  79.6 8.9 %all-to-all-done = f32[32,3,512]{2,1,0:T(4,128)S(1)} async-done(((f32[32,3,512]{2,1,0:T(4,128)}), f32[32,3,512]{2,1,0:T(4,128)S(1)}, u32[]{:S(2)}, u32[]{:S(2)}) %all-to-all-start) | async-done | bytes 196640 | tf_op jit(solution)/shard_map/all_to_all | solution.py:256
  88.9 3.8 %collective-permute-start.13 = (f32[16]{0:T(128)S(1)}, f32[16]{0:T(128)S(1)}, u32[]{:S(2)}, u32[]{:S(2)}) collective-permute-start(f32[16]{0:T(128)S(1)} %multiply_reduce_fusion), channel_id=1, source_target_pairs={{0,4},{4,0},{8,12},{12,8},{16,20},{20,16},{24,28},{28,24},{32,36},... | collective-permute-start | bytes 200 | tf_op jit(solution)/shard_map/ppermute | solution.py:36
  93.5 1.3 %collective-permute-start.14 = (f32[16]{0:T(128)S(1)}, f32[16]{0:T(128)S(1)}, u32[]{:S(2)}, u32[]{:S(2)}) collective-permute-start(f32[16]{0:T(128)S(1)} %add.65), channel_id=1, source_target_pairs={{0,1},{1,2},{2,3},{3,0},{4,5},{5,6},{6,7},{7,4},{8,9},{9,10},{10,1... | collective-permute-start | bytes 200 | tf_op jit(solution)/shard_map/ppermute | solution.py:272
  94.8 1.4 %collective-permute-start.15 = (f32[16]{0:T(128)S(1)}, f32[16]{0:T(128)S(1)}, u32[]{:S(2)}, u32[]{:S(2)}) collective-permute-start(f32[16]{0:T(128)S(1)} %add.65), channel_id=1, source_target_pairs={{0,3},{1,0},{2,1},{3,2},{4,7},{5,4},{6,5},{7,6},{8,11},{9,8},{10,9... | collective-permute-start | bytes 200 | tf_op jit(solution)/shard_map/ppermute | solution.py:272
  96.2 1.6 %collective-permute-start.16 = (f32[16]{0:T(128)S(1)}, f32[16]{0:T(128)S(1)}, u32[]{:S(2)}, u32[]{:S(2)}) collective-permute-start(f32[16]{0:T(128)S(1)} %add.65), channel_id=1, source_target_pairs={{0,2},{1,3},{2,0},{3,1},{4,6},{5,7},{6,4},{7,5},{8,10},{9,11},{10,... | collective-permute-start | bytes 200 | tf_op jit(solution)/shard_map/ppermute | solution.py:272
  97.9 2.3 %collective-permute-done.16 = f32[16]{0:T(128)S(1)} collective-permute-done((f32[16]{0:T(128)S(1)}, f32[16]{0:T(128)S(1)}, u32[]{:S(2)}, u32[]{:S(2)}) %collective-permute-start.16) | collective-permute-done | bytes 96 | tf_op jit(solution)/shard_map/ppermute | solution.py:272
  (63 shorter events, 10.6 us)
Async XLA Ops:
  0.6 78.9 %copy-start = (s32[1,4]{1,0:T(1,128)S(1)}, s32[1,4]{1,0:T(1,128)}, u32[]{:S(2)}) copy-start(s32[1,4]{1,0:T(1,128)} %param.16) | copy-start | bytes 52
  0.6 50.9 %collective-permute-start.6 = (bf16[2048,3072]{1,0:T(8,128)(2,1)}, bf16[2048,3072]{1,0:T(8,128)(2,1)}, u32[]{:S(2)}, u32[]{:S(2)}) collective-permute-start(bf16[2048,3072]{1,0:T(8,128)(2,1)} %refs_6_.1), channel_id=1, source_target_pairs={{0,4},{4,0},{8,12},{12,8},{16,20},{20,16},{24,28},{28,24},{32,36},... | collective-permute-start | bytes 37748744 | tf_op jit(solution)/shard_map/ppermute | solution.py:36
  3.9 5.8 %collective-permute-start.1 = (bf16[16,3072]{1,0:T(8,128)(2,1)}, bf16[16,3072]{1,0:T(8,128)(2,1)S(1)}, u32[]{:S(2)}, u32[]{:S(2)}) collective-permute-start(bf16[16,3072]{1,0:T(8,128)(2,1)} %bitcast.23), channel_id=1, source_target_pairs={{0,192},{4,60},{8,200},{12,4},{16,208},{20,12},{24,216},{28,20},{3... | collective-permute-start | bytes 294920 | tf_op jit(solution)/shard_map/ppermute | solution.py:31
  7.8 5.8 %collective-permute-start = (bf16[16,3072]{1,0:T(8,128)(2,1)}, bf16[16,3072]{1,0:T(8,128)(2,1)S(1)}, u32[]{:S(2)}, u32[]{:S(2)}) collective-permute-start(bf16[16,3072]{1,0:T(8,128)(2,1)} %bitcast.24), channel_id=1, source_target_pairs={{0,64},{4,12},{8,72},{12,20},{16,80},{20,28},{24,88},{28,36},{32,9... | collective-permute-start | bytes 294920 | tf_op jit(solution)/shard_map/ppermute | solution.py:31
  9.8 4.6 %collective-permute-start.2 = (bf16[16,3072]{1,0:T(8,128)(2,1)S(1)}, bf16[16,3072]{1,0:T(8,128)(2,1)S(1)}, u32[]{:S(2)}, u32[]{:S(2)}) collective-permute-start(bf16[16,3072]{1,0:T(8,128)(2,1)S(1)} %collective-permute-done.1.refs_0_), channel_id=1, source_target_pairs={{0,192},{4,60},{8,200},{12,4},{16,208},{20,12},{24,216},{28,20},{3... | collective-permute-start | bytes 294920 | tf_op jit(solution)/shard_map/ppermute | solution.py:31
  12.7 0.9 copy-start.1
  14.4 8.3 %collective-permute-start.3 = (bf16[64,3072]{1,0:T(8,128)(2,1)S(1)}, bf16[64,3072]{1,0:T(8,128)(2,1)S(1)}, u32[]{:S(2)}, u32[]{:S(2)}) collective-permute-start(bf16[64,3072]{1,0:T(8,128)(2,1)S(1)} %shard_map.142.refs_0_), channel_id=1, source_target_pairs={{0,8},{4,68},{8,16},{12,76},{16,24},{20,84},{24,32},{28,92},{32,40... | collective-permute-start | bytes 1179656 | tf_op jit(solution)/shard_map/ppermute | solution.py:31
  17.7 18.2 %collective-permute-start.4 = (bf16[64,3072]{1,0:T(8,128)(2,1)S(1)}, bf16[64,3072]{1,0:T(8,128)(2,1)S(1)}, u32[]{:S(2)}, u32[]{:S(2)}) collective-permute-start(bf16[64,3072]{1,0:T(8,128)(2,1)S(1)} %shard_map.142.refs_0_), channel_id=1, source_target_pairs={{0,56},{4,196},{8,0},{12,204},{16,8},{20,212},{24,16},{28,220},{32... | collective-permute-start | bytes 1179656 | tf_op jit(solution)/shard_map/ppermute | solution.py:31
  22.7 13.9 %collective-permute-start.5 = (bf16[64,3072]{1,0:T(8,128)(2,1)S(1)}, bf16[64,3072]{1,0:T(8,128)(2,1)S(1)}, u32[]{:S(2)}, u32[]{:S(2)}) collective-permute-start(bf16[64,3072]{1,0:T(8,128)(2,1)S(1)} %collective-permute-done.3.refs_1_), channel_id=1, source_target_pairs={{0,8},{4,68},{8,16},{12,76},{16,24},{20,84},{24,32},{28,92},{32,40... | collective-permute-start | bytes 1179656 | tf_op jit(solution)/shard_map/ppermute | solution.py:31
  23.4 12.3 %collective-permute-start.8 = (bf16[32,3072]{1,0:T(8,128)(2,1)S(1)}, bf16[32,3072]{1,0:T(8,128)(2,1)S(1)}, u32[]{:S(2)}, u32[]{:S(2)}) collective-permute-start(bf16[32,3072]{1,0:T(8,128)(2,1)S(1)} %shard_map.140.refs_0_), channel_id=1, source_target_pairs={{4,20},{12,28},{20,36},{28,44},{36,52},{44,60},{52,4},{60,12},{68,... | collective-permute-start | bytes 589832 | tf_op jit(solution)/shard_map/ppermute | solution.py:31
  25.4 10.5 %collective-permute-start.7 = (bf16[32,3072]{1,0:T(8,128)(2,1)S(1)}, bf16[32,3072]{1,0:T(8,128)(2,1)S(1)}, u32[]{:S(2)}, u32[]{:S(2)}) collective-permute-start(bf16[32,3072]{1,0:T(8,128)(2,1)S(1)} %shard_map.141.refs_1_), channel_id=1, source_target_pairs={{4,52},{12,60},{20,4},{28,12},{36,20},{44,28},{52,36},{60,44},{68,... | collective-permute-start | bytes 589832 | tf_op jit(solution)/shard_map/ppermute | solution.py:31
  35.9 3.6 %collective-permute-start.10 = (bf16[64,3072]{1,0:T(8,128)(2,1)S(1)}, bf16[64,3072]{1,0:T(8,128)(2,1)S(1)}, u32[]{:S(2)}, u32[]{:S(2)}) collective-permute-start(bf16[64,3072]{1,0:T(8,128)(2,1)S(1)} %collective-permute-done.4.refs_2_), channel_id=1, source_target_pairs={{0,56},{8,0},{16,8},{24,16},{32,24},{40,32},{48,40},{56,48},{64,12... | collective-permute-start | bytes 1179656 | tf_op jit(solution)/shard_map/ppermute | solution.py:31
  36.6 8.4 %collective-permute-start.9 = (bf16[64,3072]{1,0:T(8,128)(2,1)S(1)}, bf16[64,3072]{1,0:T(8,128)(2,1)S(1)}, u32[]{:S(2)}, u32[]{:S(2)}) collective-permute-start(bf16[64,3072]{1,0:T(8,128)(2,1)S(1)} %shard_map.146), channel_id=1, source_target_pairs={{0,8},{4,68},{8,16},{12,76},{16,24},{20,84},{24,32},{28,92},{32,40... | collective-permute-start | bytes 1179656 | tf_op jit(solution)/shard_map/ppermute | solution.py:31
  39.5 18.6 %collective-permute-start.11 = (bf16[64,3072]{1,0:T(8,128)(2,1)S(1)}, bf16[64,3072]{1,0:T(8,128)(2,1)S(1)}, u32[]{:S(2)}, u32[]{:S(2)}) collective-permute-start(bf16[64,3072]{1,0:T(8,128)(2,1)S(1)} %shard_map.147), channel_id=1, source_target_pairs={{0,56},{4,196},{8,0},{12,204},{16,8},{20,212},{24,16},{28,220},{32... | collective-permute-start | bytes 1179656 | tf_op jit(solution)/shard_map/ppermute | solution.py:31
  45.0 13.1 %collective-permute-start.12 = (bf16[64,3072]{1,0:T(8,128)(2,1)S(1)}, bf16[64,3072]{1,0:T(8,128)(2,1)S(1)}, u32[]{:S(2)}, u32[]{:S(2)}) collective-permute-start(bf16[64,3072]{1,0:T(8,128)(2,1)S(1)} %collective-permute-done.9.refs_0_), channel_id=1, source_target_pairs={{0,8},{4,68},{8,16},{12,76},{16,24},{20,84},{24,32},{28,92},{32,40... | collective-permute-start | bytes 1179656 | tf_op jit(solution)/shard_map/ppermute | solution.py:31
  58.1 21.1 %copy-start.2 = (f32[16]{0:T(128)S(1)}, f32[16]{0:T(128)}, u32[]{:S(2)}) copy-start(f32[16]{0:T(128)} %param.17) | copy-start | bytes 196
  70.4 18.1 %all-to-all-start = ((f32[32,3,512]{2,1,0:T(4,128)}), f32[32,3,512]{2,1,0:T(4,128)S(1)}, u32[]{:S(2)}, u32[]{:S(2)}) async-start(f32[32,3,512]{2,1,0:T(4,128)} %broadcast_in_dim.44), calls=%async_computation | async-start | bytes 524288 | tf_op jit(solution)/shard_map/all_to_all | solution.py:256
  88.9 4.6 %collective-permute-start.13 = (f32[16]{0:T(128)S(1)}, f32[16]{0:T(128)S(1)}, u32[]{:S(2)}, u32[]{:S(2)}) collective-permute-start(f32[16]{0:T(128)S(1)} %multiply_reduce_fusion), channel_id=1, source_target_pairs={{0,4},{4,0},{8,12},{12,8},{16,20},{20,16},{24,28},{28,24},{32,36},... | collective-permute-start | bytes 200 | tf_op jit(solution)/shard_map/ppermute | solution.py:36
  93.5 4.4 %collective-permute-start.14 = (f32[16]{0:T(128)S(1)}, f32[16]{0:T(128)S(1)}, u32[]{:S(2)}, u32[]{:S(2)}) collective-permute-start(f32[16]{0:T(128)S(1)} %add.65), channel_id=1, source_target_pairs={{0,1},{1,2},{2,3},{3,0},{4,5},{5,6},{6,7},{7,4},{8,9},{9,10},{10,1... | collective-permute-start | bytes 200 | tf_op jit(solution)/shard_map/ppermute | solution.py:272
  94.8 3.1 %collective-permute-start.15 = (f32[16]{0:T(128)S(1)}, f32[16]{0:T(128)S(1)}, u32[]{:S(2)}, u32[]{:S(2)}) collective-permute-start(f32[16]{0:T(128)S(1)} %add.65), channel_id=1, source_target_pairs={{0,3},{1,0},{2,1},{3,2},{4,7},{5,4},{6,5},{7,6},{8,11},{9,8},{10,9... | collective-permute-start | bytes 200 | tf_op jit(solution)/shard_map/ppermute | solution.py:272
  96.2 3.9 %collective-permute-start.16 = (f32[16]{0:T(128)S(1)}, f32[16]{0:T(128)S(1)}, u32[]{:S(2)}, u32[]{:S(2)}) collective-permute-start(f32[16]{0:T(128)S(1)} %add.65), channel_id=1, source_target_pairs={{0,2},{1,3},{2,0},{3,1},{4,6},{5,7},{6,4},{7,5},{8,10},{9,11},{10,... | collective-permute-start | bytes 200 | tf_op jit(solution)/shard_map/ppermute | solution.py:272

commit v3 on v2

--- a/solution.py
+++ b/solution.py
@@ -97,16 +97,17 @@
     )(own)
     r1p = move(own, (XP, ZP))
     r1m = move(own, (XM, ZM))
-    r2m = move(r1m, (XM, ZM))
-    behind, ahead = join(r1p, kept), join(r1m, r2m)
-    q0 = join(behind, ahead)
+    r2m = move(own, ((-2, 0), (0, -2)))
+    q0 = join(r1p, kept, r1m, r2m)
     q1p = move(q0, (ZP, XP))
     q1m = move(q0, (ZM, XM))
-    f3 = move(ahead, (None, (0, -2)))
-    f5 = move(behind, (None, (0, 2)))
+    r2p = move(own, (None, (0, 2)))
+    t3m = move(r2m, (None, ZM))
     q2p = move(q1p, (ZP, XP))
+    t3p = move(r2p, (None, ZP))
+    t4 = move(t3m, (None, ZM))
     q2m = move(q1m, (ZM, None))
-    far = join(f3, f5)
+    far = join(t3m, t4, t3p, r2p)
     q3p = move(pick(first, q2p, far), (ZP, XP))
     q3m = move(pick(first, q2m, far), (ZM, XM))
     q4 = move(q3p, (ZP, XP))
@@ -237,6 +238,7 @@
     to_z = (z + jnp.where(first, dz_a, dz_b)) % NZ
     to = (to_s * NZ + to_z) * rows + row
     mine = lambda a: jnp.where(first, a[:, 0], a[:, 1]).reshape(-1)
+    labels = lax.optimization_barrier(labels)
     lab = mine(labels[0].reshape(NS * NZ, NC, rows))
     hit = n[:, None] == to[None, :]
     target = jnp.sum(jnp.where(hit, lab[:, None], 0), axis=0).reshape(2, 1, 4 * 4 * rows)
@@ -258,6 +260,7 @@
     logprob = label_logit - top - jnp.log(total)
 
     slot_count = ref_logp.shape[0]
+    response_mask, ref_logp = lax.optimization_barrier((response_mask, ref_logp))
     ref_gap = ref_logp[0::2] - ref_logp[1::2]
     own_start = (s * NZ + z) * rows
     weights = response_mask[0].astype(jnp.float32).reshape(NS, NZ * NC * rows)
@@ -269,8 +272,8 @@
     token_logprob = lax.dynamic_slice_in_dim(logprob, own_start, rows, allow_negative_indices=False)[None, :]
     part = jnp.sum(by_slot * logprob[None, :], axis=1)
     part = part + swap_cores(part)
-    around = [lax.ppermute(part, "dp", [(i, (i + d) % 4) for i in range(4)]) for d in (1, 3, 2)]
-    policy = part + around[0] + around[1] + around[2]
+    part = part + lax.ppermute(part, "dp", [(i, i ^ 1) for i in range(4)])
+    policy = part + lax.ppermute(part, "dp", [(i, i ^ 3) for i in range(4)])
     pair_margin = beta_scale * (policy[0::2] - policy[1::2] - ref_gap)
     loss = jnp.mean(jnp.logaddexp(0.0, -pair_margin))
     return (token_logprob, pair_margin, loss)

time: 104 us -> 103 us (level); the launches traced: 103 us -> 101 us
  waiting for transfers between devices: 25.5 us -> 18.9 us
  starting transfers between devices: 41.1 us -> 45.4 us
    ppermute x12 -> x14, waiting for transfers between devices: 14 us -> 7.41 us  [move(): return lax.ppermute(x, PLANE, pairs)]
    ppermute x12 -> x14, starting transfers between devices: 21 us -> 27.4 us  [move(): return lax.ppermute(x, PLANE, pairs)]
    all_to_all x1, starting transfers between devices: 8.66 us -> 6.99 us  [step(): lax.all_to_all(sent, PLANE, split_axis=0, concat_axis=0, tiled=True, axis...]
    unnamed x7 -> x4, local copies, waits for them, and re-layouts: 1.42 us -> 0.02 us
    optimization_barrier x0 -> x1, other arithmetic: none -> 1.35 us  [step(): labels = lax.optimization_barrier(labels)]
    unnamed x1 -> x0, other arithmetic: 1.35 us -> none
    ppermute x3 -> x2, waiting for transfers between devices: 2.28 us -> 1.49 us  [the longest x1 1.12 us: step(): part = part + lax.ppermute(part, 'dp', [(i, i ^ 1) for i in range(4)])]
    ppermute x3 -> x2, starting transfers between devices: 4.39 us -> 4.04 us  [the longest x1 2.74 us: step(): policy = part + lax.ppermute(part, 'dp', [(i, i ^ 3) for i in range(4)])]
  transfers between devices with their start and end apart: 18 -> 19, of which waited for: 9 -> 8; matrix products, arithmetic and copies ran while one was open for 6% -> 6% of each run, Pallas kernels for 13% -> 14%
where the time goes in v3:
time: 103 us; the launch traced here: 101 us
  starting transfers between devices  45.4 us (44%)
  Pallas kernels  25 us (24%)
  waiting for transfers between devices  18.9 us (18%)
  other arithmetic  5.67 us (6%)
  local copies, waits for them, and re-layouts  2.84 us (3%)
  between operations  2.7 us (3%)
    ppermute x14, starting transfers between devices, move(): return lax.ppermute(x, PLANE, pairs)  27.4 us
    pallas_call x3, Pallas kernels, chunk_stats(): pl.pallas_call(functools.partial(stats_kernel, pieces=len(xs), heads=len(...  23.9 us
    all_to_all x1, waiting for transfers between devices, step(): lax.all_to_all(sent, PLANE, split_axis=0, concat_axis=0, tiled=True, axis...  9.14 us
    ppermute x14, waiting for transfers between devices, move(): return lax.ppermute(x, PLANE, pairs)  7.41 us
    ppermute x2, starting transfers between devices, swap_cores(): return lax.ppermute(x, PLANE, pairs)  7.01 us
    all_to_all x1, starting transfers between devices, step(): lax.all_to_all(sent, PLANE, split_axis=0, concat_axis=0, tiled=True, axis...  6.99 us
    ppermute x1, starting transfers between devices, step(): policy = part + lax.ppermute(part, 'dp', [(i, i ^ 3) for i in range(4)])  2.74 us
  transfers between devices with their start and end apart: 19, of which 8 were waited for; matrix products, arithmetic and copies ran while one was open for 6% of the time, Pallas kernels for 14%

profile of v3, /device:TPU:1, one launch (start us, length us, event | category | flops | bytes accessed | tf_op | source)
XLA Modules:
  0.0 101.0 jit_solution(18323163214933357056)
XLA Ops:
  0.6 3.3 %collective-permute-start.6 = (bf16[2048,3072]{1,0:T(8,128)(2,1)}, bf16[2048,3072]{1,0:T(8,128)(2,1)}, u32[]{:S(2)}, u32[]{:S(2)}) collective-permute-start(bf16[2048,3072]{1,0:T(8,128)(2,1)} %refs_6_.1), channel_id=1, source_target_pairs={{0,4},{4,0},{8,12},{12,8},{16,20},{20,16},{24,28},{28,24},{32,36},... | collective-permute-start | bytes 37748744 | tf_op jit(solution)/shard_map/ppermute | solution.py:36
  3.9 4.3 %collective-permute-start.2 = (bf16[16,3072]{1,0:T(8,128)(2,1)}, bf16[16,3072]{1,0:T(8,128)(2,1)S(1)}, u32[]{:S(2)}, u32[]{:S(2)}) collective-permute-start(bf16[16,3072]{1,0:T(8,128)(2,1)} %bitcast.in_ref), channel_id=1, source_target_pairs={{0,128},{4,52},{8,136},{12,60},{16,144},{20,4},{24,152},{28,12},{3... | collective-permute-start | bytes 294920 | tf_op jit(solution)/shard_map/ppermute | solution.py:31
  9.0 1.9 %collective-permute-start.1 = (bf16[16,3072]{1,0:T(8,128)(2,1)}, bf16[16,3072]{1,0:T(8,128)(2,1)S(1)}, u32[]{:S(2)}, u32[]{:S(2)}) collective-permute-start(bf16[16,3072]{1,0:T(8,128)(2,1)} %bitcast.in_ref), channel_id=1, source_target_pairs={{0,192},{4,60},{8,200},{12,4},{16,208},{20,12},{24,216},{28,20},{3... | collective-permute-start | bytes 294920 | tf_op jit(solution)/shard_map/ppermute | solution.py:31
  11.9 1.3 %collective-permute-done.refs_0_ = bf16[16,3072]{1,0:T(8,128)(2,1)S(1)} collective-permute-done((bf16[16,3072]{1,0:T(8,128)(2,1)}, bf16[16,3072]{1,0:T(8,128)(2,1)S(1)}, u32[]{:S(2)}, u32[]{:S(2)}) %collective-permute-start) | collective-permute-done | bytes 98336 | tf_op jit(solution)/shard_map/ppermute | solution.py:31
  13.2 1.3 %collective-permute-start.3 = (bf16[64,3072]{1,0:T(8,128)(2,1)S(1)}, bf16[64,3072]{1,0:T(8,128)(2,1)S(1)}, u32[]{:S(2)}, u32[]{:S(2)}) collective-permute-start(bf16[64,3072]{1,0:T(8,128)(2,1)S(1)} %shard_map.140.refs_0_), channel_id=1, source_target_pairs={{0,8},{4,68},{8,16},{12,76},{16,24},{20,84},{24,32},{28,92},{32,40... | collective-permute-start | bytes 1179656 | tf_op jit(solution)/shard_map/ppermute | solution.py:31
  14.5 1.9 %collective-permute-start.9 = (bf16[16,3072]{1,0:T(8,128)(2,1)}, bf16[16,3072]{1,0:T(8,128)(2,1)S(1)}, u32[]{:S(2)}, u32[]{:S(2)}) collective-permute-start(bf16[16,3072]{1,0:T(8,128)(2,1)} %bitcast.in_ref), channel_id=1, source_target_pairs={{4,20},{12,28},{20,36},{28,44},{36,52},{44,60},{52,4},{60,12},{68,... | collective-permute-start | bytes 294920 | tf_op jit(solution)/shard_map/ppermute | solution.py:31
  16.9 1.3 %reduce.19 = s32[1024]{0:T(1024)S(1)} reduce(s32[1,1024]{1,0:T(1,128)} %param.14, s32[]{:T(128)} %broadcast.63), dimensions={0}, to_apply=%optimization_barrier.12.reduce_sub_computation.3 | reduce | bytes 8196 | tf_op jit(solution)/shard_map/optimization_barrier | solution.py:241
  18.4 1.5 %collective-permute-start.4 = (bf16[64,3072]{1,0:T(8,128)(2,1)S(1)}, bf16[64,3072]{1,0:T(8,128)(2,1)S(1)}, u32[]{:S(2)}, u32[]{:S(2)}) collective-permute-start(bf16[64,3072]{1,0:T(8,128)(2,1)S(1)} %shard_map.140.refs_0_), channel_id=1, source_target_pairs={{0,56},{4,196},{8,0},{12,204},{16,8},{20,212},{24,16},{28,220},{32... | collective-permute-start | bytes 1179656 | tf_op jit(solution)/shard_map/ppermute | solution.py:31
  19.9 1.5 %collective-permute-done.3.refs_1_ = bf16[64,3072]{1,0:T(8,128)(2,1)S(1)} collective-permute-done((bf16[64,3072]{1,0:T(8,128)(2,1)S(1)}, bf16[64,3072]{1,0:T(8,128)(2,1)S(1)}, u32[]{:S(2)}, u32[]{:S(2)}) %collective-permute-start.3) | collective-permute-done | bytes 393248 | tf_op jit(solution)/shard_map/ppermute | solution.py:31
  22.1 4.9 %collective-permute-start.7 = (bf16[16,3072]{1,0:T(8,128)(2,1)S(1)}, bf16[16,3072]{1,0:T(8,128)(2,1)S(1)}, u32[]{:S(2)}, u32[]{:S(2)}) collective-permute-start(bf16[16,3072]{1,0:T(8,128)(2,1)S(1)} %collective-permute-done.2.refs_3_), channel_id=1, source_target_pairs={{4,60},{12,4},{20,12},{28,20},{36,28},{44,36},{52,44},{60,52},{68,... | collective-permute-start | bytes 294920 | tf_op jit(solution)/shard_map/ppermute | solution.py:31
  27.1 1.9 %collective-permute-start.10 = (bf16[16,3072]{1,0:T(8,128)(2,1)S(1)}, bf16[16,3072]{1,0:T(8,128)(2,1)S(1)}, u32[]{:S(2)}, u32[]{:S(2)}) collective-permute-start(bf16[16,3072]{1,0:T(8,128)(2,1)S(1)} %collective-permute-done.9.refs_3_), channel_id=1, source_target_pairs={{4,12},{12,20},{20,28},{28,36},{36,44},{44,52},{52,60},{60,4},{68,... | collective-permute-start | bytes 294920 | tf_op jit(solution)/shard_map/ppermute | solution.py:31
  29.1 4.6 %collective-permute-start.8 = (bf16[16,3072]{1,0:T(8,128)(2,1)S(1)}, bf16[16,3072]{1,0:T(8,128)(2,1)S(1)}, u32[]{:S(2)}, u32[]{:S(2)}) collective-permute-start(bf16[16,3072]{1,0:T(8,128)(2,1)S(1)} %collective-permute-done.7.refs_0_), channel_id=1, source_target_pairs={{4,60},{12,4},{20,12},{28,20},{36,28},{44,36},{52,44},{60,52},{68,... | collective-permute-start | bytes 294920 | tf_op jit(solution)/shard_map/ppermute | solution.py:31
  36.3 1.8 %collective-permute-start.11 = (bf16[64,3072]{1,0:T(8,128)(2,1)S(1)}, bf16[64,3072]{1,0:T(8,128)(2,1)S(1)}, u32[]{:S(2)}, u32[]{:S(2)}) collective-permute-start(bf16[64,3072]{1,0:T(8,128)(2,1)S(1)} %shard_map.144), channel_id=1, source_target_pairs={{0,8},{4,68},{8,16},{12,76},{16,24},{20,84},{24,32},{28,92},{32,40... | collective-permute-start | bytes 1179656 | tf_op jit(solution)/shard_map/ppermute | solution.py:31
  40.4 3.8 %collective-permute-done.11.refs_0_ = bf16[64,3072]{1,0:T(8,128)(2,1)S(1)} collective-permute-done((bf16[64,3072]{1,0:T(8,128)(2,1)S(1)}, bf16[64,3072]{1,0:T(8,128)(2,1)S(1)}, u32[]{:S(2)}, u32[]{:S(2)}) %collective-permute-start.11) | collective-permute-done | bytes 393248 | tf_op jit(solution)/shard_map/ppermute | solution.py:31
  45.0 6.4 %shard_map.141.refs_6_ = f32[8,256]{1,0:T(8,128)S(1)} custom-call(bf16[64,3072]{1,0:T(8,128)(2,1)S(1)} %shard_map.140.refs_0_, bf16[64,3072]{1,0:T(8,128)(2,1)S(1)} %collective-permute-done.3.refs_1_, bf16[64,3072]{1,0:T(8,128)(2,1)S(1)} %collective-permute-done.4.refs_2_, bf16[64,3072]{1,0:T(8,128)(2,1)S(1)} %collective-permute-done.5.refs_3_.mine_ref, ...), custom_call_target="tpu_custom_call" | custom-call | flops 3221225472 | bytes 12582912 | tf_op jit(solution)/shard_map/pallas_call | solution.py:184
  51.4 6.5 %shard_map.142 = f32[8,256]{1,0:T(8,128)S(1)} custom-call(bf16[64,3072]{1,0:T(8,128)(2,1)S(1)} %shard_map.140.refs_0_, bf16[64,3072]{1,0:T(8,128)(2,1)S(1)} %collective-permute-done.3.refs_1_, bf16[64,3072]{1,0:T(8,128)(2,1)S(1)} %collective-permute-done.4.refs_2_, bf16[64,3072]{1,0:T(8,128)(2,1)S(1)} %collective-permute-done.5.refs_3_.mine_ref, ...), custom_call_target="tpu_custom_call" | custom-call | flops 3221225472 | bytes 12582912 | tf_op jit(solution)/shard_map/pallas_call | solution.py:184
  57.9 11.0 %shard_map.146 = f32[8,256]{1,0:T(8,128)S(1)} custom-call(bf16[64,3072]{1,0:T(8,128)(2,1)S(1)} %collective-permute-done.11.refs_0_, bf16[64,3072]{1,0:T(8,128)(2,1)S(1)} %collective-permute-done.13.refs_1_, bf16[64,3072]{1,0:T(8,128)(2,1)S(1)} %collective-permute-done.14.refs_2_, bf16[64,3072]{1,0:T(8,128)(2,1)S(1)} %collective-permute-done.12.mine_ref.refs_3_, ...), custom_call_target="tpu_custom_call" | custom-call | flops 6442450944 | bytes 25165824 | tf_op jit(solution)/shard_map/pallas_call | solution.py:184
  70.2 7.0 %all-to-all-start = ((f32[32,3,512]{2,1,0:T(4,128)}), f32[32,3,512]{2,1,0:T(4,128)S(1)}, u32[]{:S(2)}, u32[]{:S(2)}) async-start(f32[32,3,512]{2,1,0:T(4,128)} %broadcast_in_dim.44), calls=%async_computation | async-start | bytes 524288 | tf_op jit(solution)/shard_map/all_to_all | solution.py:258
  77.8 9.1 %all-to-all-done = f32[32,3,512]{2,1,0:T(4,128)S(1)} async-done(((f32[32,3,512]{2,1,0:T(4,128)}), f32[32,3,512]{2,1,0:T(4,128)S(1)}, u32[]{:S(2)}, u32[]{:S(2)}) %all-to-all-start) | async-done | bytes 196640 | tf_op jit(solution)/shard_map/all_to_all | solution.py:258
  87.3 3.7 %collective-permute-start.15 = (f32[16]{0:T(128)S(1)}, f32[16]{0:T(128)S(1)}, u32[]{:S(2)}, u32[]{:S(2)}) collective-permute-start(f32[16]{0:T(128)S(1)} %multiply_reduce_fusion), channel_id=1, source_target_pairs={{0,4},{4,0},{8,12},{12,8},{16,20},{20,16},{24,28},{28,24},{32,36},... | collective-permute-start | bytes 200 | tf_op jit(solution)/shard_map/ppermute | solution.py:36
  91.8 1.3 %collective-permute-start.16 = (f32[16]{0:T(128)S(1)}, f32[16]{0:T(128)S(1)}, u32[]{:S(2)}, u32[]{:S(2)}) collective-permute-start(f32[16]{0:T(128)S(1)} %add.62), channel_id=1, source_target_pairs={{0,1},{1,0},{2,3},{3,2},{4,5},{5,4},{6,7},{7,6},{8,9},{9,8},{10,11... | collective-permute-start | bytes 200 | tf_op jit(solution)/shard_map/ppermute | solution.py:275
  93.1 1.1 %collective-permute-done.16 = f32[16]{0:T(128)S(1)} collective-permute-done((f32[16]{0:T(128)S(1)}, f32[16]{0:T(128)S(1)}, u32[]{:S(2)}, u32[]{:S(2)}) %collective-permute-start.16) | collective-permute-done | bytes 96 | tf_op jit(solution)/shard_map/ppermute | solution.py:275
  94.2 2.7 %collective-permute-start.17 = (f32[16]{0:T(128)S(1)}, f32[16]{0:T(128)S(1)}, u32[]{:S(2)}, u32[]{:S(2)}) collective-permute-start(f32[16]{0:T(128)S(1)} %add.63), channel_id=1, source_target_pairs={{0,3},{1,2},{2,1},{3,0},{4,7},{5,6},{6,5},{7,4},{8,11},{9,10},{10,... | collective-permute-start | bytes 200 | tf_op jit(solution)/shard_map/ppermute | solution.py:276
  98.1 1.1 %fusion.17 = (f32[]{:T(128)}, f32[8]{0:T(128)}) fusion(f32[8]{0:T(128)S(1)} %slice.47, f32[8]{0:T(128)S(1)} %slice.48, f32[8]{0:T(128)S(1)} %slice.45, f32[8]{0:T(128)S(1)} %slice.46), kind=kLoop, calls=%fused_computation.36 | loop fusion | flops 103 | bytes 164 | tf_op jit(solution)/shard_map/reduce_sum | solution.py:278
  (62 shorter events, 13.0 us)
Async XLA Ops:
  0.6 77.1 %copy-start = (s32[1,4]{1,0:T(1,128)S(1)}, s32[1,4]{1,0:T(1,128)}, u32[]{:S(2)}) copy-start(s32[1,4]{1,0:T(1,128)} %param.16) | copy-start | bytes 52
  0.6 50.7 %collective-permute-start.6 = (bf16[2048,3072]{1,0:T(8,128)(2,1)}, bf16[2048,3072]{1,0:T(8,128)(2,1)}, u32[]{:S(2)}, u32[]{:S(2)}) collective-permute-start(bf16[2048,3072]{1,0:T(8,128)(2,1)} %refs_6_.1), channel_id=1, source_target_pairs={{0,4},{4,0},{8,12},{12,8},{16,20},{20,16},{24,28},{28,24},{32,36},... | collective-permute-start | bytes 37748744 | tf_op jit(solution)/shard_map/ppermute | solution.py:36
  3.9 7.9 %collective-permute-start.2 = (bf16[16,3072]{1,0:T(8,128)(2,1)}, bf16[16,3072]{1,0:T(8,128)(2,1)S(1)}, u32[]{:S(2)}, u32[]{:S(2)}) collective-permute-start(bf16[16,3072]{1,0:T(8,128)(2,1)} %bitcast.in_ref), channel_id=1, source_target_pairs={{0,128},{4,52},{8,136},{12,60},{16,144},{20,4},{24,152},{28,12},{3... | collective-permute-start | bytes 294920 | tf_op jit(solution)/shard_map/ppermute | solution.py:31
  8.2 4.9 %collective-permute-start = (bf16[16,3072]{1,0:T(8,128)(2,1)}, bf16[16,3072]{1,0:T(8,128)(2,1)S(1)}, u32[]{:S(2)}, u32[]{:S(2)}) collective-permute-start(bf16[16,3072]{1,0:T(8,128)(2,1)} %bitcast.in_ref), channel_id=1, source_target_pairs={{0,64},{4,12},{8,72},{12,20},{16,80},{20,28},{24,88},{28,36},{32,9... | collective-permute-start | bytes 294920 | tf_op jit(solution)/shard_map/ppermute | solution.py:31
  9.0 4.2 %collective-permute-start.1 = (bf16[16,3072]{1,0:T(8,128)(2,1)}, bf16[16,3072]{1,0:T(8,128)(2,1)S(1)}, u32[]{:S(2)}, u32[]{:S(2)}) collective-permute-start(bf16[16,3072]{1,0:T(8,128)(2,1)} %bitcast.in_ref), channel_id=1, source_target_pairs={{0,192},{4,60},{8,200},{12,4},{16,208},{20,12},{24,216},{28,20},{3... | collective-permute-start | bytes 294920 | tf_op jit(solution)/shard_map/ppermute | solution.py:31
  13.2 8.2 %collective-permute-start.3 = (bf16[64,3072]{1,0:T(8,128)(2,1)S(1)}, bf16[64,3072]{1,0:T(8,128)(2,1)S(1)}, u32[]{:S(2)}, u32[]{:S(2)}) collective-permute-start(bf16[64,3072]{1,0:T(8,128)(2,1)S(1)} %shard_map.140.refs_0_), channel_id=1, source_target_pairs={{0,8},{4,68},{8,16},{12,76},{16,24},{20,84},{24,32},{28,92},{32,40... | collective-permute-start | bytes 1179656 | tf_op jit(solution)/shard_map/ppermute | solution.py:31
  14.5 12.7 %collective-permute-start.9 = (bf16[16,3072]{1,0:T(8,128)(2,1)}, bf16[16,3072]{1,0:T(8,128)(2,1)S(1)}, u32[]{:S(2)}, u32[]{:S(2)}) collective-permute-start(bf16[16,3072]{1,0:T(8,128)(2,1)} %bitcast.in_ref), channel_id=1, source_target_pairs={{4,20},{12,28},{20,36},{28,44},{36,52},{44,60},{52,4},{60,12},{68,... | collective-permute-start | bytes 294920 | tf_op jit(solution)/shard_map/ppermute | solution.py:31
  18.4 17.1 %collective-permute-start.4 = (bf16[64,3072]{1,0:T(8,128)(2,1)S(1)}, bf16[64,3072]{1,0:T(8,128)(2,1)S(1)}, u32[]{:S(2)}, u32[]{:S(2)}) collective-permute-start(bf16[64,3072]{1,0:T(8,128)(2,1)S(1)} %shard_map.140.refs_0_), channel_id=1, source_target_pairs={{0,56},{4,196},{8,0},{12,204},{16,8},{20,212},{24,16},{28,220},{32... | collective-permute-start | bytes 1179656 | tf_op jit(solution)/shard_map/ppermute | solution.py:31
  21.4 14.8 %collective-permute-start.5 = (bf16[64,3072]{1,0:T(8,128)(2,1)S(1)}, bf16[64,3072]{1,0:T(8,128)(2,1)S(1)}, u32[]{:S(2)}, u32[]{:S(2)}) collective-permute-start(bf16[64,3072]{1,0:T(8,128)(2,1)S(1)} %collective-permute-done.3.refs_1_), channel_id=1, source_target_pairs={{0,8},{4,68},{8,16},{12,76},{16,24},{20,84},{24,32},{28,92},{32,40... | collective-permute-start | bytes 1179656 | tf_op jit(solution)/shard_map/ppermute | solution.py:31
  22.1 7.0 %collective-permute-start.7 = (bf16[16,3072]{1,0:T(8,128)(2,1)S(1)}, bf16[16,3072]{1,0:T(8,128)(2,1)S(1)}, u32[]{:S(2)}, u32[]{:S(2)}) collective-permute-start(bf16[16,3072]{1,0:T(8,128)(2,1)S(1)} %collective-permute-done.2.refs_3_), channel_id=1, source_target_pairs={{4,60},{12,4},{20,12},{28,20},{36,28},{44,36},{52,44},{60,52},{68,... | collective-permute-start | bytes 294920 | tf_op jit(solution)/shard_map/ppermute | solution.py:31
  27.1 7.5 %collective-permute-start.10 = (bf16[16,3072]{1,0:T(8,128)(2,1)S(1)}, bf16[16,3072]{1,0:T(8,128)(2,1)S(1)}, u32[]{:S(2)}, u32[]{:S(2)}) collective-permute-start(bf16[16,3072]{1,0:T(8,128)(2,1)S(1)} %collective-permute-done.9.refs_3_), channel_id=1, source_target_pairs={{4,12},{12,20},{20,28},{28,36},{36,44},{44,52},{52,60},{60,4},{68,... | collective-permute-start | bytes 294920 | tf_op jit(solution)/shard_map/ppermute | solution.py:31
  29.1 6.4 %collective-permute-start.8 = (bf16[16,3072]{1,0:T(8,128)(2,1)S(1)}, bf16[16,3072]{1,0:T(8,128)(2,1)S(1)}, u32[]{:S(2)}, u32[]{:S(2)}) collective-permute-start(bf16[16,3072]{1,0:T(8,128)(2,1)S(1)} %collective-permute-done.7.refs_0_), channel_id=1, source_target_pairs={{4,60},{12,4},{20,12},{28,20},{36,28},{44,36},{52,44},{60,52},{68,... | collective-permute-start | bytes 294920 | tf_op jit(solution)/shard_map/ppermute | solution.py:31
  35.5 3.8 %collective-permute-start.12 = (bf16[64,3072]{1,0:T(8,128)(2,1)S(1)}, bf16[64,3072]{1,0:T(8,128)(2,1)S(1)}, u32[]{:S(2)}, u32[]{:S(2)}) collective-permute-start(bf16[64,3072]{1,0:T(8,128)(2,1)S(1)} %collective-permute-done.4.refs_2_), channel_id=1, source_target_pairs={{0,56},{8,0},{16,8},{24,16},{32,24},{40,32},{48,40},{56,48},{64,12... | collective-permute-start | bytes 1179656 | tf_op jit(solution)/shard_map/ppermute | solution.py:31
  36.3 7.9 %collective-permute-start.11 = (bf16[64,3072]{1,0:T(8,128)(2,1)S(1)}, bf16[64,3072]{1,0:T(8,128)(2,1)S(1)}, u32[]{:S(2)}, u32[]{:S(2)}) collective-permute-start(bf16[64,3072]{1,0:T(8,128)(2,1)S(1)} %shard_map.144), channel_id=1, source_target_pairs={{0,8},{4,68},{8,16},{12,76},{16,24},{20,84},{24,32},{28,92},{32,40... | collective-permute-start | bytes 1179656 | tf_op jit(solution)/shard_map/ppermute | solution.py:31
  39.3 18.6 %collective-permute-start.13 = (bf16[64,3072]{1,0:T(8,128)(2,1)S(1)}, bf16[64,3072]{1,0:T(8,128)(2,1)S(1)}, u32[]{:S(2)}, u32[]{:S(2)}) collective-permute-start(bf16[64,3072]{1,0:T(8,128)(2,1)S(1)} %shard_map.145), channel_id=1, source_target_pairs={{0,56},{4,196},{8,0},{12,204},{16,8},{20,212},{24,16},{28,220},{32... | collective-permute-start | bytes 1179656 | tf_op jit(solution)/shard_map/ppermute | solution.py:31
  44.2 13.7 %collective-permute-start.14 = (bf16[64,3072]{1,0:T(8,128)(2,1)S(1)}, bf16[64,3072]{1,0:T(8,128)(2,1)S(1)}, u32[]{:S(2)}, u32[]{:S(2)}) collective-permute-start(bf16[64,3072]{1,0:T(8,128)(2,1)S(1)} %collective-permute-done.11.refs_0_), channel_id=1, source_target_pairs={{0,8},{4,68},{8,16},{12,76},{16,24},{20,84},{24,32},{28,92},{32,40... | collective-permute-start | bytes 1179656 | tf_op jit(solution)/shard_map/ppermute | solution.py:31
  57.9 19.5 %copy-start.1 = (f32[16]{0:T(128)S(1)}, f32[16]{0:T(128)}, u32[]{:S(2)}) copy-start(f32[16]{0:T(128)} %param.17) | copy-start | bytes 196
  70.2 16.7 %all-to-all-start = ((f32[32,3,512]{2,1,0:T(4,128)}), f32[32,3,512]{2,1,0:T(4,128)S(1)}, u32[]{:S(2)}, u32[]{:S(2)}) async-start(f32[32,3,512]{2,1,0:T(4,128)} %broadcast_in_dim.44), calls=%async_computation | async-start | bytes 524288 | tf_op jit(solution)/shard_map/all_to_all | solution.py:258
  87.3 4.5 %collective-permute-start.15 = (f32[16]{0:T(128)S(1)}, f32[16]{0:T(128)S(1)}, u32[]{:S(2)}, u32[]{:S(2)}) collective-permute-start(f32[16]{0:T(128)S(1)} %multiply_reduce_fusion), channel_id=1, source_target_pairs={{0,4},{4,0},{8,12},{12,8},{16,20},{20,16},{24,28},{28,24},{32,36},... | collective-permute-start | bytes 200 | tf_op jit(solution)/shard_map/ppermute | solution.py:36
  91.8 2.4 %collective-permute-start.16 = (f32[16]{0:T(128)S(1)}, f32[16]{0:T(128)S(1)}, u32[]{:S(2)}, u32[]{:S(2)}) collective-permute-start(f32[16]{0:T(128)S(1)} %add.62), channel_id=1, source_target_pairs={{0,1},{1,0},{2,3},{3,2},{4,5},{5,4},{6,7},{7,6},{8,9},{9,8},{10,11... | collective-permute-start | bytes 200 | tf_op jit(solution)/shard_map/ppermute | solution.py:275
  94.2 3.7 %collective-permute-start.17 = (f32[16]{0:T(128)S(1)}, f32[16]{0:T(128)S(1)}, u32[]{:S(2)}, u32[]{:S(2)}) collective-permute-start(f32[16]{0:T(128)S(1)} %add.63), channel_id=1, source_target_pairs={{0,3},{1,2},{2,1},{3,0},{4,7},{5,6},{6,5},{7,4},{8,11},{9,10},{10,... | collective-permute-start | bytes 200 | tf_op jit(solution)/shard_map/ppermute | solution.py:276
